TPU v7x, 256 devices: a 4x2x16 block of a 4x16x16 slice. The times are simulated.
256 devices in a mesh: groups: 2 (over y), frame: 64 (over x, z), row: 2 (over core).
Axes of the slice: x: 4, y: 2, z: 16, core: 2. Of those that a mesh axis runs over, the one named last changes fastest.
The devices are a block of a 4x16x16 slice.
Arguments:
- latent: bfloat16 [128, 16, 64, 640], P(('groups', 'frame'), 'row'), parts along dimension 0, may hold values from -18 to 18
- norm_gain: float32 [640], replicated, may hold values from 0.1 to 1.9
- time_kernel: bfloat16 [3, 640, 640], replicated, may hold values from -0.125 to 0.125
- space_norm: float32 [640], replicated, may hold values from 0.1 to 1.9
- space_qkv: bfloat16 [640, 1920], replicated, may hold values from -12 to 12
- space_out: bfloat16 [640, 640], replicated, may hold values from -0.25 to 0.25
- time_norm: float32 [640], replicated, may hold values from 0.1 to 1.9
- time_qkv: bfloat16 [640, 1920], replicated, may hold values from -12 to 12
- time_out: bfloat16 [640, 640], replicated, may hold values from -0.25 to 0.25
Outputs:
- output: float32 [128, 16, 64, 640], P(('groups', 'frame'), 'row'), parts along dimension 0
There are 2 independent parts, one for each index of `groups`. A program takes and returns all parts, laid end to end along the dimension named above; an argument that names none is the same for every part. Nothing has to cross between parts.
All inputs are finite; a program needn't handle non-finite values.
Results may differ from a plain program's by a relative error of at most 0.0018.
Values may be sent and summed in bfloat16 or wider, within the bound.
No kernel may reach another device: no remote copies, remote signals or barrier semaphores. Data moves between devices by JAX's collectives and lax.ppermute only.
A program may use at most 128 MiB of HBM per device.

v0:
```python
import functools

import jax
import jax.numpy as jnp
from jax import lax
from jax.sharding import Mesh
from jax.sharding import PartitionSpec as P

HEADS = 10
GROUPS = 32
FRAME_ROW = ("frame_0", "frame_1", "row")
FRAME = ("frame_0", "frame_1")
GROUPS_FRAME = ("groups", "frame_0", "frame_1")


epsilon = 1e-05


def over_axes(x, axes):
    return functools.reduce(lax.psum, axes, x)


def padded_2(block, sides, width):
    for axis, dim in sides:
        count = lax.axis_size(axis)
        forward = [(i, i + 1) for i in range(count - 1)]
        backward = [(target, source) for source, target in forward]
        low = lax.ppermute(
            lax.slice_in_dim(block, block.shape[dim] - width, None, axis=dim), axis, forward
        )
        high = lax.ppermute(lax.slice_in_dim(block, 0, width, axis=dim), axis, backward)
        block = jnp.concatenate([low, block, high], axis=dim)
    return block


def sent_together(arrays, axis, split_dim, concat_dim, along):
    both = jnp.concatenate(arrays, axis=along)
    whole, at, done = (
        lax.all_to_all(both, axis, split_axis=split_dim, concat_axis=concat_dim, tiled=True),
        0,
        [],
    )
    for a in arrays:
        done.append(lax.slice_in_dim(whole, at, at + a.shape[along], axis=along))
        at += a.shape[along]
    return tuple(done)


def normalize_silu(grouped, first, second, number, gain, shape):
    center = first / number
    spread = second / number - center * center
    scaling = lax.rsqrt(spread + epsilon)
    normed = ((grouped - center[:, None]) * scaling[:, None]).reshape(shape) * gain
    return jax.nn.silu(normed).astype(jnp.bfloat16)


def layer_norm(inputs, gain):
    center = jnp.mean(inputs, axis=-1, keepdims=True)
    shifted = inputs - center
    spread = jnp.mean(shifted * shifted, axis=-1, keepdims=True)
    return (shifted * lax.rsqrt(spread + epsilon) * gain).astype(jnp.bfloat16)


def project_three(inputs, weight):
    channels = weight.shape[0]
    lead = inputs.shape[:-1]
    packed = jnp.dot(
        inputs.reshape(-1, channels), weight, preferred_element_type=jnp.float32
    ).astype(jnp.bfloat16)
    packed = packed.reshape(lead + (3 * channels,))
    return (
        packed[..., :channels],
        packed[..., channels : 2 * channels],
        packed[..., 2 * channels :],
    )


def frame_attend(queries, key_rows, values, heads):
    frames, length, width_local = queries.shape
    head_size = width_local // heads
    query_heads = queries.reshape(frames, length, heads, head_size)
    key_heads = key_rows.reshape(frames, length, heads, head_size)
    value_heads = values.reshape(frames, length, heads, head_size)
    scores = jnp.einsum(
        "fqhd,fkhd->fhqk", query_heads, key_heads, preferred_element_type=jnp.float32
    ) * head_size ** (-0.5)
    raised = jnp.exp(scores - jnp.max(scores, axis=-1, keepdims=True))
    weight_sum = jnp.sum(raised, axis=-1)
    weights = raised.astype(jnp.bfloat16)
    result = jnp.einsum("fhqk,fkhd->fqhd", weights, value_heads, preferred_element_type=jnp.float32)
    result = result / jnp.transpose(weight_sum, (0, 2, 1))[:, :, :, None]
    return result.astype(jnp.bfloat16).reshape(frames, length, width_local)


def time_attend(queries, key_rows, values):
    frames, pixels, channels = queries.shape
    head_size = channels // HEADS
    query_heads = queries.reshape(frames, pixels, HEADS, head_size)
    key_heads = key_rows.reshape(frames, pixels, HEADS, head_size)
    value_heads = values.reshape(frames, pixels, HEADS, head_size)
    scores = jnp.einsum(
        "qphd,kphd->phqk", query_heads, key_heads, preferred_element_type=jnp.float32
    ) * head_size ** (-0.5)
    raised = jnp.exp(scores - jnp.max(scores, axis=-1, keepdims=True))
    weight_sum = jnp.sum(raised, axis=-1)
    weights = raised.astype(jnp.bfloat16)
    result = jnp.einsum("phqk,kphd->qphd", weights, value_heads, preferred_element_type=jnp.float32)
    result = result / jnp.transpose(weight_sum, (2, 0, 1))[:, :, :, None]
    return result.astype(jnp.bfloat16).reshape(frames, pixels, channels)


def add_projected(base, attended, weight):
    channels = weight.shape[0]
    summed = base.reshape(-1, channels) + jnp.dot(
        attended.reshape(-1, channels), weight, preferred_element_type=jnp.float32
    )
    return summed.reshape(base.shape)


def body(
    latent, norm_gain, time_kernel, space_norm, space_qkv, space_out, time_norm, time_qkv, time_out
):
    frames, row_count, col_count, channels = latent.shape
    pixels = row_count * col_count
    per_group = channels // GROUPS
    grouped = latent.astype(jnp.float32).reshape(frames, row_count, col_count, GROUPS, per_group)
    first = jnp.sum(grouped, axis=(0, 1, 2, 4))
    second = jnp.sum(grouped * grouped, axis=(0, 1, 2, 4))
    first, second = (over_axes(first, FRAME_ROW), over_axes(second, FRAME_ROW))
    number = frames * lax.axis_size(FRAME) * pixels * lax.axis_size("row") * per_group
    hidden = normalize_silu(grouped, first, second, number, norm_gain, latent.shape)
    padded = padded_2(hidden, ((FRAME, 0),), 1)
    mixed = jnp.zeros((frames * pixels, channels), jnp.float32)
    for tap in range(3):
        window = padded[tap : tap + frames].reshape(-1, channels)
        mixed = mixed + jnp.dot(window, time_kernel[tap], preferred_element_type=jnp.float32)
    stepped = latent.astype(jnp.float32).reshape(-1, channels) + mixed
    stepped = stepped.reshape(frames, pixels, channels)
    tokens = layer_norm(stepped, space_norm)
    queries, key_rows, values = project_three(tokens, space_qkv)
    moved = sent_together((queries, key_rows, values), "row", 2, 1, 0)
    local_heads = HEADS // lax.axis_size("row")
    result = frame_attend(moved[0], moved[1], moved[2], local_heads)
    attended = lax.all_to_all(result, "row", split_axis=1, concat_axis=2, tiled=True)
    spaced = add_projected(stepped, attended, space_out)
    moved = lax.all_to_all(spaced, FRAME, split_axis=1, concat_axis=0, tiled=True)
    normed = layer_norm(moved, time_norm)
    queries, key_rows, values = project_three(normed, time_qkv)
    result = time_attend(queries, key_rows, values)
    finished = add_projected(moved, result, time_out)
    output = lax.all_to_all(finished, FRAME, split_axis=0, concat_axis=1, tiled=True)
    return output.reshape(frames, row_count, col_count, channels)


def solution(mesh):
    finer = Mesh(
        mesh.devices.reshape(mesh.shape["groups"], 4, 16, mesh.shape["row"]),
        ("groups", "frame_0", "frame_1", "row"),
    )
    placed = (P(GROUPS_FRAME, "row", None, None), P(), P(), P(), P(), P(), P(), P(), P())
    return jax.shard_map(
        body,
        mesh=finer,
        in_specs=placed,
        out_specs=P(GROUPS_FRAME, "row", None, None),
        check_vma=False,
    )
```

profile of v0, /device:TPU:38, one launch (start us, length us, event | category | flops | bytes accessed | tf_op | source)
XLA Modules:
  0.0 322.7 jit_solution(7806964619746096641)
XLA Ops:
  0.0 1.4 convert_reduce_fusion
  1.9 25.6 %all-reduce.1 = (f32[32]{0:T(128)S(1)}, f32[32]{0:T(128)S(1)}) all-reduce(f32[32]{0:T(128)S(1)} %reduce_sum.93, f32[32]{0:T(128)S(1)} %reduce_sum.90), channel_id=1, replica_groups=mesh['groups'=2,'frame_0'=4,'frame_1'=16,'row'=2] {'frame_0'}, use_global_device_ids=true, to_apply=%region_7.0 | all-reduce | flops 64 | bytes 512 | tf_op jit(solution)/shard_map/psum | solution.py:20
  27.5 31.3 %all-reduce = (f32[32]{0:T(128)S(1)}, f32[32]{0:T(128)S(1)}) all-reduce(f32[32]{0:T(128)S(1)} %get-tuple-element.9, f32[32]{0:T(128)S(1)} %get-tuple-element.10), channel_id=1, replica_groups=mesh['groups'=2,'frame_0'=4,'frame_1'=16,'row'=2] {'frame_1'}, use_global_device_ids=true, to_apply=%region_8.9 | all-reduce | flops 64 | bytes 512 | tf_op jit(solution)/shard_map/psum | solution.py:20
  58.8 2.5 all-reduce.2
  61.7 1.5 multiply_convert_fusion.1
  63.2 2.8 collective-permute-start.1
  66.0 3.1 collective-permute-start
  69.1 2.0 fusion.26
  71.2 10.7 %collective-permute-done.1 = bf16[1,8,64,640]{3,2,1,0:T(8,128)(2,1)S(1)} collective-permute-done((bf16[1,8,64,640]{3,2,1,0:T(8,128)(2,1)S(1)}, bf16[1,8,64,640]{3,2,1,0:T(8,128)(2,1)S(1)}, u32[]{:S(2)}, u32[]{:S(2)}) %collective-permute-start.1) | collective-permute-done | bytes 655392 | tf_op jit(solution)/shard_map/ppermute | solution.py:31
  81.9 0.8 fusion.24
  82.7 3.9 %collective-permute-done = bf16[1,8,64,640]{3,2,1,0:T(8,128)(2,1)S(1)} collective-permute-done((bf16[1,8,64,640]{3,2,1,0:T(8,128)(2,1)S(1)}, bf16[1,8,64,640]{3,2,1,0:T(8,128)(2,1)S(1)}, u32[]{:S(2)}, u32[]{:S(2)}) %collective-permute-start) | collective-permute-done | bytes 655392 | tf_op jit(solution)/shard_map/ppermute | solution.py:28
  86.6 0.9 fusion.44
  88.2 1.9 fusion.4
  90.2 1.5 pad_maximum_fusion
  91.8 4.2 %copy.41 = bf16[3,512,640]{1,0,2:T(4,128)(2,1)S(1)} copy(bf16[3,512,640]{2,1,0:T(8,128)(2,1)} %pad_maximum_fusion) | data formatting | bytes 3932160 | tf_op jit(solution)/shard_map/concatenate | solution.py:37
  96.0 6.0 %all_to_all.48 = bf16[3,512,640]{1,0,2:T(4,128)(2,1)S(1)} all-to-all(bf16[3,512,640]{1,0,2:T(4,128)(2,1)S(1)} %copy.41), channel_id=1, replica_groups=mesh['groups'=2,'frame_0'=4,'frame_1'=16,'row'=2] {'row'}, dimensions={2} | all-to-all | bytes 3932160 | tf_op jit(solution)/shard_map/all_to_all | solution.py:39
  103.3 1.3 reshape.192
  105.3 1.3 reshape.193
  107.3 1.3 reshape.194
  108.6 4.2 %multiply_reduce_fusion = (f32[5,1024]{1,0:T(8,128)S(1)}, f32[5,1024,1024]{1,2,0:T(8,128)S(1)}) fusion(bf16[1024,5,64]{0,2,1:T(8,128)(2,1)} %reshape.193, bf16[1024,5,64]{0,2,1:T(8,128)(2,1)} %reshape.194), kind=kOutput, calls=%fused_computation.1 | convolution fusion | flops 681569280 | bytes 22302720 | tf_op jit(solution)/shard_map/fqhd,fkhd->fhqk/dot_general | solution.py:84
  112.8 4.3 %fusion = f32[5,1024]{1,0:T(8,128)} fusion(f32[5,1024,1024]{1,2,0:T(8,128)S(1)} %get-tuple-element.27, f32[5,1024]{1,0:T(8,128)S(1)} %get-tuple-element.26), kind=kLoop, calls=%fused_computation.2 | loop fusion | flops 15723520 | bytes 21012480 | tf_op jit(solution)/shard_map/reduce_sum | solution.py:88
  117.1 5.6 %divide_convert_fusion = bf16[1,1024,5,64]{1,3,2,0:T(8,128)(2,1)} fusion(bf16[1024,5,64]{0,2,1:T(8,128)(2,1)} %reshape.192, f32[5,1024,1024]{1,2,0:T(8,128)S(1)} %get-tuple-element.27, f32[5,1024]{1,0:T(8,128)S(1)} %get-tuple-element.26, f32[1024,5]{0,1:T(8,128)} %bitcast.99), kind=kOutput, calls=%fused_computation.31 | convolution fusion | flops 687472640 | bytes 22323200 | tf_op jit(solution)/shard_map/fhqk,fkhd->fqhd/dot_general | solution.py:90
  122.6 4.3 %copy.47 = bf16[1,1024,320]{2,0,1:T(2,128)(2,1)S(1)} copy(bf16[1,1024,320]{1,2,0:T(8,128)(2,1)} %bitcast.92) | data formatting | bytes 1310720 | tf_op jit(solution)/shard_map/reshape | solution.py:92
  127.5 5.8 %reduce.15 = bf16[1024,320]{1,0:T(8,128)(2,1)S(1)} reduce(bf16[1024,1,320]{2,1,0:T(2,128)(2,1)S(1)} %bitcast.85, bf16[]{:T(256)} %broadcast.96), dimensions={1}, to_apply=%bitcast.65.reduce_sub_computation | reduce | bytes 1310722
  133.3 0.9 reshape.206
  134.2 4.3 %all_to_all.49 = bf16[2,2,81920]{2,1,0:T(2,128)(2,1)S(1)} all-to-all(bf16[2,2,81920]{2,1,0:T(2,128)(2,1)S(1)} %reshape.206), channel_id=1, replica_groups=mesh['groups'=2,'frame_0'=4,'frame_1'=16,'row'=2] {'row'}, dimensions={0} | all-to-all | bytes 1310720 | tf_op jit(solution)/shard_map/all_to_all | solution.py:144
  138.5 1.3 reshape.207
  140.0 0.9 copy.62
  141.3 0.8 copy-done.7
  142.1 0.8 fusion.11
  142.9 1.3 copy.50
  144.2 72.1 %all_to_all.50 = f32[1,512,640]{2,0,1:T(1,128)S(1)} all-to-all(f32[1,512,640]{2,0,1:T(1,128)S(1)} %copy.50), channel_id=1, replica_groups=mesh['groups'=2,'frame_0'=4,'frame_1'=16,'row'=2] {'frame_0','frame_1'}, dimensions={1} | all-to-all | bytes 2621440 | tf_op jit(solution)/shard_map/all_to_all | solution.py:146
  216.3 1.6 reduce_sum.98
  217.9 7.6 %multiply_reduce_fusion.2 = f32[512]{0:T(512)S(1)} fusion(f32[1,512,640]{2,0,1:T(1,128)S(1)} %all_to_all.50, f32[512]{0:T(512)S(1)} %broadcast_multiply_fusion), kind=kLoop, calls=%fused_computation.30 | loop fusion | flops 982528 | bytes 1314816 | tf_op jit(solution)/shard_map/reduce_sum | solution.py:60
  225.6 3.6 %fusion.5 = bf16[64,8,1920]{2,1,0:T(8,128)(2,1)S(1)} fusion(bf16[640,1920]{1,0:T(8,128)(2,1)} %param.16, f32[1,512,640]{2,0,1:T(1,128)S(1)} %all_to_all.50, f32[640]{0:T(1024)S(1)} %copy-done.9, f32[512]{0:T(512)S(1)} %add_rsqrt_fusion, f32[512]{0:T(512)S(1)} %broadcast_multiply_fusion), kind=kOutput, calls=%fused_computation.8 | convolution fusion | flops 1260584960 | bytes 5741056 | tf_op jit(solution)/shard_map/dot_general | solution.py:67
  229.2 1.0 fusion.41
  230.2 1.6 copy.51
  231.7 2.0 copy.65
  233.7 1.6 copy.66
  235.3 2.0 multiply_reduce_fusion.1
  237.3 0.7 fusion.7
  238.6 1.8 fusion.6
  240.4 3.5 %copy.57 = bf16[64,8,10,64]{3,2,1,0:T(8,128)(2,1)S(1)} copy(bf16[64,8,10,64]{0,3,2,1:T(8,128)(2,1)} %fusion.6) | data formatting | bytes 1310720 | tf_op jit(solution)/shard_map/convert_element_type | solution.py:109
  243.9 1.9 reshape_reshape.3
  245.8 2.1 fusion.12
  247.9 72.2 %all_to_all.51 = f32[64,8,640]{2,1,0:T(8,128)S(1)} all-to-all(f32[64,8,640]{2,1,0:T(8,128)S(1)} %fusion.12), channel_id=1, replica_groups=mesh['groups'=2,'frame_0'=4,'frame_1'=16,'row'=2] {'frame_0','frame_1'}, dimensions={0} | all-to-all | bytes 2621440 | tf_op jit(solution)/shard_map/all_to_all | solution.py:151
  320.1 1.1 copy.71
  321.2 1.1 copy-done.1
  (41 shorter events, 6.0 us)
Async XLA Ops:
  0.0 87.8 %copy-start = (bf16[640,1920]{1,0:T(8,128)(2,1)S(1)}, bf16[640,1920]{1,0:T(8,128)(2,1)}, u32[]{:S(2)}) copy-start(bf16[640,1920]{1,0:T(8,128)(2,1)} %param.13) | copy-start | bytes 7372804
  63.2 18.7 %collective-permute-start.1 = (bf16[1,8,64,640]{3,2,1,0:T(8,128)(2,1)S(1)}, bf16[1,8,64,640]{3,2,1,0:T(8,128)(2,1)S(1)}, u32[]{:S(2)}, u32[]{:S(2)}) collective-permute-start(bf16[1,8,64,640]{3,2,1,0:T(8,128)(2,1)S(1)} %multiply_convert_fusion.1), channel_id=1, source_target_pairs={{2,0},{4,2},{6,4},{8,6},{10,8},{12,10},{14,12},{16,14},{18,16},{20... | collective-permute-start | bytes 1966088 | tf_op jit(solution)/shard_map/ppermute | solution.py:31
  66.0 20.6 %collective-permute-start = (bf16[1,8,64,640]{3,2,1,0:T(8,128)(2,1)S(1)}, bf16[1,8,64,640]{3,2,1,0:T(8,128)(2,1)S(1)}, u32[]{:S(2)}, u32[]{:S(2)}) collective-permute-start(bf16[1,8,64,640]{3,2,1,0:T(8,128)(2,1)S(1)} %multiply_convert_fusion.1), channel_id=1, source_target_pairs={{0,2},{2,4},{4,6},{6,8},{8,10},{10,12},{12,14},{14,16},{16,18},{18... | collective-permute-start | bytes 1966088 | tf_op jit(solution)/shard_map/ppermute | solution.py:28
  69.1 12.8 %copy-start.5 = (bf16[3,640,640]{2,1,0:T(8,128)(2,1)S(1)}, bf16[3,640,640]{2,1,0:T(8,128)(2,1)}, u32[]{:S(2)}) copy-start(bf16[3,640,640]{2,1,0:T(8,128)(2,1)} %param.11) | copy-start | bytes 7372804
  81.9 4.6 %copy-start.4 = (bf16[1,8,64,640]{3,2,1,0:T(8,128)(2,1)S(1)}, bf16[1,8,64,640]{3,2,1,0:T(8,128)(2,1)}, u32[]{:S(2)}) copy-start(bf16[1,8,64,640]{3,2,1,0:T(8,128)(2,1)} %param.9) | copy-start | bytes 1966084
  87.5 2.6 copy-start.2
  87.5 0.7 copy-start.8
  140.0 1.3 copy-start.3
  140.8 1.2 copy-start.7
  216.3 9.3 %copy-start.9 = (f32[640]{0:T(1024)S(1)}, f32[640]{0:T(1024)}, u32[]{:S(2)}) copy-start(f32[640]{0:T(1024)} %param.15) | copy-start | bytes 7684
  237.3 1.3 copy-start.6
  320.1 2.2 copy-start.1
where the time goes:
time: 329 us; the launch traced here: 323 us
  blocking collectives  214 us (65%)
  local copies, waits for them, and re-layouts  36.9 us (11%)
  matrix products  25.5 us (8%)
  other arithmetic  25.1 us (8%)
  waiting for transfers between devices  14.6 us (4%)
  starting transfers between devices  5.9 us (2%)
    all_to_all x1, blocking collectives, body(): lax.all_to_all(finished, FRAME, split_axis=0, concat_axis=1, tiled=True)  72.2 us
    all_to_all x1, blocking collectives, body(): lax.all_to_all(spaced, FRAME, split_axis=1, concat_axis=0, tiled=True)  72.1 us
    psum x3, blocking collectives, over_axes(): return functools.reduce(lax.psum, axes, x)  59.4 us
    unnamed x27, local copies, waits for them, and re-layouts  10.8 us
    ppermute x1, waiting for transfers between devices, padded_2(): lax.ppermute(lax.slice_in_dim(block, 0, width, axis=dim), axis, backward)  10.7 us
    reduce_sum x2, other arithmetic, layer_norm(): spread = jnp.mean(shifted * shifted, axis=-1, keepdims=True)  7.93 us
  transfers between devices with their start and end apart: 2, of which 2 were waited for; matrix products, arithmetic and copies ran while one was open for 1% of the time, Pallas kernels for 0%

commit v1 on v0

v1 whole, which is shorter than its diff:
```python
import functools

import jax
import jax.numpy as jnp
from jax import lax
from jax.experimental import pallas as pl
from jax.experimental.pallas import tpu as pltpu
from jax.sharding import PartitionSpec as P

HEADS = 10
GROUPS = 32
FRAME = "frame"
FRAME_ROW = ("frame", "row")
LOG2E = 1.4426950408889634

epsilon = 1e-05
f32 = jnp.float32
bf16 = jnp.bfloat16


def vmem():
    return pl.BlockSpec(memory_space=pltpu.VMEM)


def params(mib):
    return pltpu.CompilerParams(vmem_limit_bytes=mib << 20)


def cost(flops, nbytes, trans=0):
    return pl.CostEstimate(flops=flops, bytes_accessed=nbytes, transcendentals=trans)


def dot(a, b, dims=((1,), (0,)), precision=None):
    return lax.dot_general(
        a, b, (dims, ((), ())), preferred_element_type=f32, precision=precision
    )


def group_slots(channels, offset):
    per_group = channels // GROUPS
    slot = lax.broadcasted_iota(jnp.int32, (128, channels), 0)
    chan = lax.broadcasted_iota(jnp.int32, (128, channels), 1)
    low = (slot - offset) * per_group
    inside = (chan >= low) & (chan < low + per_group)
    return jnp.where(inside, 1.0, 0.0).astype(f32)


def layer_norm(inputs, gain):
    center = jnp.mean(inputs, axis=-1, keepdims=True)
    shifted = inputs - center
    spread = jnp.mean(shifted * shifted, axis=-1, keepdims=True)
    return (shifted * lax.rsqrt(spread + epsilon) * gain).astype(bf16)


def sums_kernel(x_ref, o_ref, acc):
    step = pl.program_id(0)
    x = x_ref[...].astype(f32)
    rows, channels = x.shape
    part = x.reshape(rows // 8, 8, channels)
    first, second = jnp.sum(part, axis=0), jnp.sum(part * part, axis=0)

    @pl.when(step == 0)
    def _():
        acc[0] = first
        acc[1] = second

    @pl.when(step > 0)
    def _():
        acc[0] += first
        acc[1] += second

    @pl.when(step == pl.num_programs(0) - 1)
    def _():
        exact = lax.Precision.HIGHEST
        total = dot(acc[0], group_slots(channels, 0), ((1,), (1,)), exact)
        total += dot(acc[1], group_slots(channels, GROUPS), ((1,), (1,)), exact)
        row = jnp.sum(total, axis=0, keepdims=True)
        o_ref[...] = jnp.broadcast_to(row[None], o_ref.shape)


def group_sums(latent, members):
    rows, channels = latent.shape
    tile = rows // 2
    return pl.pallas_call(
        sums_kernel,
        out_shape=jax.ShapeDtypeStruct((members, 1, 128), f32),
        grid=(rows // tile,),
        in_specs=[pl.BlockSpec((tile, channels), lambda i: (i, 0))],
        out_specs=pl.BlockSpec((members, 1, 128), lambda i: (0, 0, 0)),
        scratch_shapes=[pltpu.VMEM((2, 8, channels), f32)],
        compiler_params=params(16),
        cost_estimate=cost(4 * rows * channels, 2 * rows * channels),
        name="group_sums",
    )(latent)


def front_kernel(
    number, edge_ref, sums_ref, gain_ref, low_ref, mid_ref, high_ref, kernel_ref, norm_ref,
    stepped_ref, tokens_ref, scale
):
    channels = mid_ref.shape[1]

    @pl.when(pl.program_id(0) == 0)
    def _():
        exact = lax.Precision.HIGHEST
        total = jnp.broadcast_to(jnp.sum(sums_ref[...], axis=0), (8, 128))
        center = dot(total, group_slots(channels, 0), precision=exact) / number
        square = dot(total, group_slots(channels, GROUPS), precision=exact) / number
        scaling = lax.rsqrt(square - center * center + epsilon) * gain_ref[...]
        scale[0] = scaling
        scale[1] = center

    scaling, center = scale[0, 0:1], scale[1, 0:1]

    def hidden(ref):
        half = 0.5 * ((ref[...].astype(f32) - center) * scaling)
        return (half + half * jnp.tanh(half)).astype(bf16)

    low = hidden(low_ref)
    low = jnp.where(edge_ref[0] > 0, low, jnp.zeros_like(low))
    high = hidden(high_ref)
    high = jnp.where(edge_ref[1] > 0, high, jnp.zeros_like(high))
    mixed = dot(low, kernel_ref[0])
    mixed += dot(hidden(mid_ref), kernel_ref[1])
    mixed += dot(high, kernel_ref[2])
    stepped = mid_ref[...].astype(f32) + mixed
    stepped_ref[...] = stepped
    tokens_ref[...] = layer_norm(stepped, norm_ref[...])


def front(edge, sums, gain, low, mid, high, time_kernel, norm, number):
    rows, channels = mid.shape
    tile = rows // 2
    block = pl.BlockSpec((tile, channels), lambda i: (i, 0))
    one = pl.BlockSpec((1, channels), lambda i: (0, 0))
    return pl.pallas_call(
        functools.partial(front_kernel, number),
        out_shape=[
            jax.ShapeDtypeStruct((rows, channels), f32),
            jax.ShapeDtypeStruct((rows, channels), bf16),
        ],
        grid=(rows // tile,),
        in_specs=[
            pl.BlockSpec(memory_space=pltpu.SMEM),
            vmem(),
            one,
            block,
            block,
            block,
            vmem(),
            one,
        ],
        out_specs=[block, block],
        scratch_shapes=[pltpu.VMEM((2, 8, channels), f32)],
        compiler_params=params(24),
        cost_estimate=cost(6 * rows * channels * channels, 14 * rows * channels),
        name="front",
    )(edge, sums, gain, low, mid, high, time_kernel, norm)


def half_masks(shape):
    lane = lax.broadcasted_iota(jnp.int32, shape, len(shape) - 1)
    even = jnp.where(lane < 64, 1.0, 0.0).astype(bf16)
    odd = jnp.where(lane < 64, 0.0, 1.0).astype(bf16)
    return even, odd


def space_kernel(
    own_ref, peer_ref, stepped_ref, qkv_ref, out_ref, norm_ref, spaced_ref, normed_ref,
    queries, keys, values, attended
):
    rows, channels = own_ref.shape
    pairs = channels // 128
    length = 2 * rows
    even, odd = half_masks((rows, 128))
    for half, ref in enumerate((own_ref, peer_ref)):
        packed = dot(ref[...], qkv_ref[:, channels:]).astype(bf16)
        at = half * rows
        for j in range(pairs):
            k = packed[:, j * 128 : j * 128 + 128]
            v = packed[:, channels + j * 128 : channels + j * 128 + 128]
            for part, mask in enumerate((even, odd)):
                low = part * length + at
                keys[j, low : low + rows] = k * mask
                values[j, low : low + rows, :128] = v * mask
                values[j, low : low + rows, 128:] = mask
    packed = dot(own_ref[...], qkv_ref[:, :channels]).astype(bf16)
    for j in range(pairs):
        queries[j] = packed[:, j * 128 : j * 128 + 128]

    factor = 64 ** (-0.5) * LOG2E

    def pair(j, carry):
        q = queries[j]
        total = None
        for part in range(2):
            low = part * length
            scores = dot(q, keys[j, low : low + length], ((1,), (1,)))
            top = jnp.max(scores, axis=-1, keepdims=True)
            weights = jnp.exp2((scores - top) * factor).astype(bf16)
            found = dot(weights, values[j, low : low + length])
            total = found if total is None else total + found
        attended[j] = (total[:, :128] / total[:, 128:]).astype(bf16)
        return carry

    lax.fori_loop(0, pairs, pair, 0)
    joined = jnp.concatenate([attended[j] for j in range(pairs)], axis=1)
    spaced = stepped_ref[...] + dot(joined, out_ref[...])
    spaced_ref[...] = spaced
    normed_ref[...] = layer_norm(spaced, norm_ref[...])


def space(own, peer, stepped, qkv, out, norm):
    rows, channels = own.shape
    pairs = channels // 128
    return pl.pallas_call(
        space_kernel,
        out_shape=[
            jax.ShapeDtypeStruct((rows, channels), f32),
            jax.ShapeDtypeStruct((rows, channels), bf16),
        ],
        in_specs=[vmem()] * 6,
        out_specs=[vmem()] * 2,
        scratch_shapes=[
            pltpu.VMEM((pairs, rows, 128), bf16),
            pltpu.VMEM((pairs, 4 * rows, 128), bf16),
            pltpu.VMEM((pairs, 4 * rows, 256), bf16),
            pltpu.VMEM((pairs, rows, 128), bf16),
        ],
        compiler_params=params(40),
        cost_estimate=cost(12 * rows * channels * channels + 8 * rows * rows * channels, 14 * rows * channels, 2 * HEADS * rows * rows),
        name="space",
    )(own, peer, stepped, qkv, out, norm)


def time_kernel_body(x_ref, qkv_ref, o_ref, packed_ref, attended):
    frames, pixels, channels = x_ref.shape
    rows = frames * pixels
    pairs = channels // 128
    i = lax.broadcasted_iota(jnp.int32, (rows, rows), 0)
    j = lax.broadcasted_iota(jnp.int32, (rows, rows), 1)
    order = (j == (i % frames) * pixels + i // frames).astype(f32).astype(bf16)
    sorted_rows = dot(order, x_ref[...].reshape(rows, channels)).astype(bf16)
    packed_ref[...] = dot(sorted_rows, qkv_ref[...]).astype(bf16)
    factor = 64 ** (-0.5) * LOG2E
    even, odd = half_masks((frames, 128))
    left = lax.broadcasted_iota(jnp.int32, (frames, 128), 1) < 64
    low = jnp.full((frames, 128), -jnp.inf, f32)

    def pixel(p, carry):
        at = pl.multiple_of(p * frames, frames)
        for j in range(pairs):
            q = packed_ref[pl.ds(at, frames), j * 128 : j * 128 + 128]
            k = packed_ref[pl.ds(at, frames), channels + j * 128 : channels + j * 128 + 128]
            v = packed_ref[
                pl.ds(at, frames), 2 * channels + j * 128 : 2 * channels + j * 128 + 128
            ]
            scores = dot(q, jnp.concatenate([k * even, k * odd], axis=0), ((1,), (1,)))
            top_even = jnp.max(jnp.where(left, scores, low), axis=-1, keepdims=True)
            top_odd = jnp.max(jnp.where(left, low, scores), axis=-1, keepdims=True)
            top = jnp.where(left, top_even, top_odd)
            weights = jnp.exp2((scores - top) * factor).astype(bf16)
            both = jnp.concatenate(
                [
                    jnp.concatenate([v * even, even], axis=1),
                    jnp.concatenate([v * odd, odd], axis=1),
                ],
                axis=0,
            )
            found = dot(weights, both)
            attended[pl.ds(at, frames), j * 128 : j * 128 + 128] = (
                found[:, :128] / found[:, 128:]
            ).astype(bf16)
        return carry

    lax.fori_loop(0, pixels, pixel, 0)
    back = dot(order, attended[...], ((0,), (0,))).astype(bf16)
    o_ref[...] = back.reshape(frames, pixels, channels)


def time_attend(x, qkv):
    frames, pixels, channels = x.shape
    rows = frames * pixels
    return pl.pallas_call(
        time_kernel_body,
        out_shape=jax.ShapeDtypeStruct(x.shape, bf16),
        in_specs=[vmem()] * 2,
        out_specs=vmem(),
        scratch_shapes=[
            pltpu.VMEM((rows, 3 * channels), bf16),
            pltpu.VMEM((rows, channels), bf16),
        ],
        compiler_params=params(32),
        cost_estimate=cost(6 * rows * channels * channels + 4 * rows * rows * channels, 4 * rows * channels, HEADS * rows * frames),
        name="time_attend",
    )(x, qkv)


def finish_kernel(base_ref, x_ref, w_ref, o_ref):
    o_ref[...] = base_ref[...] + dot(x_ref[...], w_ref[...])


def finish(base, x, w):
    rows, channels = base.shape
    tile = rows // 4
    block = pl.BlockSpec((tile, channels), lambda i: (i, 0))
    return pl.pallas_call(
        finish_kernel,
        out_shape=jax.ShapeDtypeStruct((rows, channels), f32),
        grid=(rows // tile,),
        in_specs=[block, block, vmem()],
        out_specs=block,
        compiler_params=params(16),
        cost_estimate=cost(2 * rows * channels * channels, 10 * rows * channels),
        name="finish",
    )(base, x, w)


def body(
    latent, norm_gain, time_kernel, space_norm, space_qkv, space_out, time_norm, time_qkv, time_out
):
    frames, row_count, col_count, channels = latent.shape
    pixels = row_count * col_count
    assert frames == 1
    mine = latent.reshape(pixels, channels)
    count = lax.axis_size(FRAME)
    forward = [(i, i + 1) for i in range(count - 1)]
    backward = [(target, source) for source, target in forward]
    low = lax.ppermute(mine, FRAME, forward)
    high = lax.ppermute(mine, FRAME, backward)
    members = lax.axis_size(FRAME_ROW)
    sums = group_sums(mine, members)
    sums = lax.all_to_all(sums, FRAME_ROW, split_axis=0, concat_axis=0, tiled=True)
    number = float(members * pixels * (channels // GROUPS))
    here = lax.axis_index(FRAME)
    edge = jnp.stack([here > 0, here < count - 1]).astype(jnp.int32)
    stepped, tokens = front(
        edge, sums, norm_gain.reshape(1, -1), low, mine, high, time_kernel,
        space_norm.reshape(1, -1), number,
    )
    peer = lax.ppermute(tokens, "row", [(0, 1), (1, 0)])
    spaced, normed = space(tokens, peer, stepped, space_qkv, space_out, time_norm.reshape(1, -1))
    moved = lax.all_to_all(
        normed.reshape(count, pixels // count, channels),
        FRAME, split_axis=0, concat_axis=0, tiled=True,
    )
    result = time_attend(moved, time_qkv)
    back = lax.all_to_all(result, FRAME, split_axis=0, concat_axis=0, tiled=True)
    output = finish(spaced, back.reshape(pixels, channels), time_out)
    return output.reshape(frames, row_count, col_count, channels)


def solution(mesh):
    split = P(("groups", "frame"), "row", None, None)
    return jax.shard_map(
        body,
        mesh=mesh,
        in_specs=(split,) + (P(),) * 8,
        out_specs=split,
        check_vma=False,
    )
```

time: 329 us -> 184 us (0.56); the launches traced: 323 us -> 184 us
  blocking collectives: 214 us -> 89 us
  Pallas kernels: 0 us -> 37.7 us
  starting transfers between devices: 5.9 us -> 39.6 us
  local copies, waits for them, and re-layouts: 36.9 us -> 5.27 us
  matrix products: 25.5 us -> 0 us
  other arithmetic: 25.1 us -> 0.07 us
    all_to_all x4 -> x2, blocking collectives: 155 us -> 89 us  [the longest x1 45.1 us: body(): lax.all_to_all(normed.reshape(count, pixels // count, channels), FRAME, s...]
    psum x3 -> x0, blocking collectives: 59.4 us -> none  [over_axes(): return functools.reduce(lax.psum, axes, x)]
    pallas_call x0 -> x5, Pallas kernels: none -> 37.7 us  [the longest x1 16.2 us: space(): pl.pallas_call(space_kernel, out_shape=[jax.ShapeDtypeStruct((rows, chann...]
    dot_general x11 -> x0, matrix products: 25.5 us -> none  [the longest x1 5.56 us: frame_attend(): jnp.einsum('fhqk,fkhd->fqhd', weights, value_heads, preferred_element_typ...]
    ppermute x2 -> x3, starting transfers between devices: 5.9 us -> 26.7 us  [the longest x1 24.4 us: body(): high = lax.ppermute(mine, FRAME, backward)]
    reduce_sum x8 -> x0, other arithmetic: 16.2 us -> none  [the longest x2 7.93 us: layer_norm(): spread = jnp.mean(shifted * shifted, axis=-1, keepdims=True)]
    all_to_all x0 -> x1, starting transfers between devices: none -> 12.9 us  [body(): lax.all_to_all(sums, FRAME_ROW, split_axis=0, concat_axis=0, tiled=True)]
    ppermute x2 -> x3, waiting for transfers between devices: 14.6 us -> 2.05 us  [the longest x1 2.05 us: body(): peer = lax.ppermute(tokens, 'row', [(0, 1), (1, 0)])]
  transfers between devices with their start and end apart: 2 -> 4, of which waited for: 2 -> 2; matrix products, arithmetic and copies ran while one was open for 1% -> 1% of each run, Pallas kernels for 0% -> 1%
where the time goes in v1:
time: 184 us
  blocking collectives  89 us (48%)
  starting transfers between devices  39.6 us (22%)
  Pallas kernels  37.7 us (20%)
  waiting for transfers between devices  12.2 us (7%)
  local copies, waits for them, and re-layouts  5.27 us (3%)
    all_to_all x1, blocking collectives, body(): lax.all_to_all(normed.reshape(count, pixels // count, channels), FRAME, s...  45.1 us
    all_to_all x1, blocking collectives, body(): lax.all_to_all(result, FRAME, split_axis=0, concat_axis=0, tiled=True)  43.9 us
    ppermute x1, starting transfers between devices, body(): high = lax.ppermute(mine, FRAME, backward)  24.4 us
    pallas_call x1, Pallas kernels, space(): pl.pallas_call(space_kernel, out_shape=[jax.ShapeDtypeStruct((rows, chann...  16.2 us
    pallas_call x1, Pallas kernels, time_attend(): pl.pallas_call(time_kernel_body, out_shape=jax.ShapeDtypeStruct(x.shape,...  13.4 us
    all_to_all x1, starting transfers between devices, body(): lax.all_to_all(sums, FRAME_ROW, split_axis=0, concat_axis=0, tiled=True)  12.9 us
    all_to_all x1, waiting for transfers between devices, body(): lax.all_to_all(sums, FRAME_ROW, split_axis=0, concat_axis=0, tiled=True)  10.2 us
    pallas_call x1, Pallas kernels, front(): pl.pallas_call(functools.partial(front_kernel, number), out_shape=[jax.Sh...  4.04 us
  transfers between devices with their start and end apart: 4, of which 2 were waited for; matrix products, arithmetic and copies ran while one was open for 1% of the time, Pallas kernels for 1%

profile of v1, /device:TPU:38, one launch (start us, length us, event | category | flops | bytes accessed | tf_op | source)
XLA Modules:
  0.0 184.0 jit_solution(10983472638074567053)
XLA Ops:
  0.0 24.4 %collective-permute-start.1 = (bf16[512,640]{1,0:T(8,128)(2,1)}, bf16[512,640]{1,0:T(8,128)(2,1)S(1)}, u32[]{:S(2)}, u32[]{:S(2)}) collective-permute-start(bf16[512,640]{1,0:T(8,128)(2,1)} %bitcast.7), channel_id=1, source_target_pairs={{2,0},{4,2},{6,4},{8,6},{10,8},{12,10},{14,12},{16,14},{18,16},{20... | collective-permute-start | bytes 1966088 | tf_op jit(solution)/shard_map/ppermute | solution.py:330
  24.4 2.0 %collective-permute-start = (bf16[512,640]{1,0:T(8,128)(2,1)}, bf16[512,640]{1,0:T(8,128)(2,1)S(1)}, u32[]{:S(2)}, u32[]{:S(2)}) collective-permute-start(bf16[512,640]{1,0:T(8,128)(2,1)} %bitcast.8), channel_id=1, source_target_pairs={{0,2},{2,4},{4,6},{6,8},{8,10},{10,12},{12,14},{14,16},{16,18},{18... | collective-permute-start | bytes 1966088 | tf_op jit(solution)/shard_map/ppermute | solution.py:329
  26.4 0.0 copy-start.1
  26.4 1.1 copy-done.1
  27.5 0.0 copy-start.6
  27.5 1.7 group_sums.1
  29.2 0.0 copy-start.7
  29.2 12.9 %all-to-all-start = ((f32[128,1,128]{2,1,0:T(1,128)}), f32[128,1,128]{2,1,0:T(1,128)S(1)}, u32[]{:S(2)}, u32[]{:S(2)}) async-start(f32[128,1,128]{2,1,0:T(1,128)} %group_sums.1), calls=%async_computation | async-start | bytes 131072 | tf_op jit(solution)/shard_map/all_to_all | solution.py:333
  42.1 0.7 reshape.22.gain_ref
  42.8 0.7 reshape.23.norm_ref
  43.5 0.1 add_convert_fusion.edge_ref
  43.6 10.2 %all-to-all-done.sums_ref = f32[128,1,128]{2,1,0:T(1,128)S(1)} async-done(((f32[128,1,128]{2,1,0:T(1,128)}), f32[128,1,128]{2,1,0:T(1,128)S(1)}, u32[]{:S(2)}, u32[]{:S(2)}) %all-to-all-start) | async-done | bytes 65568 | tf_op jit(solution)/shard_map/all_to_all | solution.py:333
  53.7 0.0 collective-permute-done.1.high_ref
  53.7 0.0 collective-permute-done.low_ref
  53.8 0.0 copy-start.2
  53.8 1.1 copy-done.2
  54.8 0.0 copy-start.3
  54.8 1.7 copy-done.3
  56.5 0.0 copy-start.4
  56.5 4.0 %front.1 = (f32[512,640]{1,0:T(8,128)S(1)}, bf16[512,640]{1,0:T(8,128)(2,1)S(1)}) custom-call(s32[2]{0:T(128)S(1)} %add_convert_fusion.edge_ref, f32[128,1,128]{2,1,0:T(1,128)S(1)} %all-to-all-done.sums_ref, f32[1,640]{1,0:T(1,128)S(1)} %reshape.22.gain_ref, bf16[512,640]{1,0:T(8,128)(2,1)S(1)} %collective-permute-done.low_ref, ...), custom_call_target="tpu_custom_call" | custom-call | flops 1258291200 | bytes 4587520 | tf_op jit(solution)/shard_map/front/pallas_call | solution.py:136
  60.6 0.3 collective-permute-start.2
  60.9 0.0 copy-done.7
  60.9 2.0 %collective-permute-done.2.peer_ref = bf16[512,640]{1,0:T(8,128)(2,1)S(1)} collective-permute-done((bf16[512,640]{1,0:T(8,128)(2,1)S(1)}, bf16[512,640]{1,0:T(8,128)(2,1)S(1)}, u32[]{:S(2)}, u32[]{:S(2)}) %collective-permute-start.2) | collective-permute-done | bytes 655392 | tf_op jit(solution)/shard_map/ppermute | solution.py:341
  63.0 0.0 copy-done.6
  63.0 0.0 copy-done.4
  63.0 0.0 copy-start.5
  63.0 16.2 %space.1 = (f32[512,640]{1,0:T(8,128)S(1)}, bf16[512,640]{1,0:T(8,128)(2,1)S(1)}) custom-call(bf16[512,640]{1,0:T(8,128)(2,1)S(1)} %get-tuple-element.9.own_ref, bf16[512,640]{1,0:T(8,128)(2,1)S(1)} %collective-permute-done.2.peer_ref, f32[512,640]{1,0:T(8,128)S(1)} %get-tuple-element.10.stepped_ref, bf16[640,1920]{1,0:T(8,128)(2,1)S(1)} %copy-done.4, ...), custom_call_target="tpu_custom_call" | custom-call | flops 3858759680 | bytes 4587520 | tf_op jit(solution)/shard_map/space/pallas_call | solution.py:216
  79.2 45.1 %all_to_all.15.x_ref = bf16[64,8,640]{2,1,0:T(8,128)(2,1)S(1)} all-to-all(bf16[64,8,640]{2,1,0:T(8,128)(2,1)S(1)} %bitcast.11), channel_id=1, replica_groups=mesh['groups'=2,'frame'=64,'row'=2] {'frame'}, dimensions={0} | all-to-all | bytes 1310720 | tf_op jit(solution)/shard_map/all_to_all | solution.py:343
  124.3 0.0 copy-done.5
  124.3 0.0 copy-start
  124.3 13.4 %time_attend.1 = bf16[64,8,640]{2,1,0:T(8,128)(2,1)S(1)} custom-call(bf16[64,8,640]{2,1,0:T(8,128)(2,1)S(1)} %all_to_all.15.x_ref, bf16[640,1920]{1,0:T(8,128)(2,1)S(1)} %copy-done.5), custom_call_target="tpu_custom_call" | custom-call | flops 1929379840 | bytes 1310720 | tf_op jit(solution)/shard_map/time_attend/pallas_call | solution.py:284
  137.7 43.9 %all_to_all.16 = bf16[64,8,640]{2,1,0:T(8,128)(2,1)S(1)} all-to-all(bf16[64,8,640]{2,1,0:T(8,128)(2,1)S(1)} %time_attend.1), channel_id=1, replica_groups=mesh['groups'=2,'frame'=64,'row'=2] {'frame'}, dimensions={0} | all-to-all | bytes 1310720 | tf_op jit(solution)/shard_map/all_to_all | solution.py:348
  181.6 0.0 copy-done
  181.6 2.4 %finish.1 = f32[512,640]{1,0:T(8,128)} custom-call(f32[512,640]{1,0:T(8,128)S(1)} %get-tuple-element.11.base_ref, bf16[512,640]{1,0:T(8,128)(2,1)S(1)} %bitcast.6, bf16[640,640]{1,0:T(8,128)(2,1)S(1)} %copy-done), custom_call_target="tpu_custom_call" | custom-call | flops 419430400 | bytes 3276800 | tf_op jit(solution)/shard_map/finish/pallas_call | solution.py:307
  (1 shorter events, 0.0 us)
Async XLA Ops:
  0.0 53.7 %collective-permute-start.1 = (bf16[512,640]{1,0:T(8,128)(2,1)}, bf16[512,640]{1,0:T(8,128)(2,1)S(1)}, u32[]{:S(2)}, u32[]{:S(2)}) collective-permute-start(bf16[512,640]{1,0:T(8,128)(2,1)} %bitcast.7), channel_id=1, source_target_pairs={{2,0},{4,2},{6,4},{8,6},{10,8},{12,10},{14,12},{16,14},{18,16},{20... | collective-permute-start | bytes 1966088 | tf_op jit(solution)/shard_map/ppermute | solution.py:330
  24.4 29.3 %collective-permute-start = (bf16[512,640]{1,0:T(8,128)(2,1)}, bf16[512,640]{1,0:T(8,128)(2,1)S(1)}, u32[]{:S(2)}, u32[]{:S(2)}) collective-permute-start(bf16[512,640]{1,0:T(8,128)(2,1)} %bitcast.8), channel_id=1, source_target_pairs={{0,2},{2,4},{4,6},{6,8},{8,10},{10,12},{12,14},{14,16},{16,18},{18... | collective-permute-start | bytes 1966088 | tf_op jit(solution)/shard_map/ppermute | solution.py:329
  26.4 1.1 copy-start.1
  27.5 35.5 %copy-start.6 = (bf16[640,640]{1,0:T(8,128)(2,1)S(1)}, bf16[640,640]{1,0:T(8,128)(2,1)}, u32[]{:S(2)}) copy-start(bf16[640,640]{1,0:T(8,128)(2,1)} %out_ref.1) | copy-start | bytes 2457604
  29.2 31.8 %copy-start.7 = (f32[640]{0:T(1024)S(1)}, f32[640]{0:T(1024)}, u32[]{:S(2)}) copy-start(f32[640]{0:T(1024)} %param.15) | copy-start | bytes 7684
  29.2 24.6 %all-to-all-start = ((f32[128,1,128]{2,1,0:T(1,128)}), f32[128,1,128]{2,1,0:T(1,128)S(1)}, u32[]{:S(2)}, u32[]{:S(2)}) async-start(f32[128,1,128]{2,1,0:T(1,128)} %group_sums.1), calls=%async_computation | async-start | bytes 131072 | tf_op jit(solution)/shard_map/all_to_all | solution.py:333
  53.8 1.1 copy-start.2
  54.8 1.7 copy-start.3
  56.5 6.5 %copy-start.4 = (bf16[640,1920]{1,0:T(8,128)(2,1)S(1)}, bf16[640,1920]{1,0:T(8,128)(2,1)}, u32[]{:S(2)}) copy-start(bf16[640,1920]{1,0:T(8,128)(2,1)} %qkv_ref.2) | copy-start | bytes 7372804
  60.6 2.4 %collective-permute-start.2 = (bf16[512,640]{1,0:T(8,128)(2,1)S(1)}, bf16[512,640]{1,0:T(8,128)(2,1)S(1)}, u32[]{:S(2)}, u32[]{:S(2)}) collective-permute-start(bf16[512,640]{1,0:T(8,128)(2,1)S(1)} %get-tuple-element.9.own_ref), channel_id=1, source_target_pairs={{0,1},{1,0},{2,3},{3,2},{4,5},{5,4},{6,7},{7,6},{8,9},{9,8},{10,11... | collective-permute-start | bytes 1966088 | tf_op jit(solution)/shard_map/ppermute | solution.py:341
  63.0 61.3 %copy-start.5 = (bf16[640,1920]{1,0:T(8,128)(2,1)S(1)}, bf16[640,1920]{1,0:T(8,128)(2,1)}, u32[]{:S(2)}) copy-start(bf16[640,1920]{1,0:T(8,128)(2,1)} %qkv_ref.3) | copy-start | bytes 7372804
  124.3 57.3 %copy-start = (bf16[640,640]{1,0:T(8,128)(2,1)S(1)}, bf16[640,640]{1,0:T(8,128)(2,1)}, u32[]{:S(2)}) copy-start(bf16[640,640]{1,0:T(8,128)(2,1)} %w_ref.1) | copy-start | bytes 2457604

commit v2 on v1

--- a/solution.py
+++ b/solution.py
@@ -178,32 +178,33 @@
         at = half * rows
         for j in range(pairs):
             k = packed[:, j * 128 : j * 128 + 128]
-            v = packed[:, channels + j * 128 : channels + j * 128 + 128]
-            for part, mask in enumerate((even, odd)):
-                low = part * length + at
-                keys[j, low : low + rows] = k * mask
-                values[j, low : low + rows, :128] = v * mask
-                values[j, low : low + rows, 128:] = mask
+            keys[j, at : at + rows] = k * even
+            keys[j, length + at : length + at + rows] = k * odd
+            v = packed[:, channels + j * 128 : channels + j * 128 + 128].T
+            values[j, :128, at : at + rows] = v
+            values[j, 128:, at : at + rows] = jnp.ones((16, rows), bf16)
     packed = dot(own_ref[...], qkv_ref[:, :channels]).astype(bf16)
     for j in range(pairs):
-        queries[j] = packed[:, j * 128 : j * 128 + 128]
+        queries[j] = packed[:, j * 128 : j * 128 + 128].T
 
     factor = 64 ** (-0.5) * LOG2E
 
     def pair(j, carry):
         q = queries[j]
-        total = None
+        weights = []
         for part in range(2):
             low = part * length
-            scores = dot(q, keys[j, low : low + length], ((1,), (1,)))
-            top = jnp.max(scores, axis=-1, keepdims=True)
-            weights = jnp.exp2((scores - top) * factor).astype(bf16)
-            found = dot(weights, values[j, low : low + length])
-            total = found if total is None else total + found
-        attended[j] = (total[:, :128] / total[:, 128:]).astype(bf16)
+            scores = dot(keys[j, low : low + length], q)
+            top = jnp.max(scores, axis=0, keepdims=True)
+            weights.append(jnp.exp2((scores - top) * factor).astype(bf16))
+        first = dot(values[j], weights[0])
+        second = dot(values[j], weights[1])
+        first = first[:64] / first[128:129]
+        second = second[64:128] / second[128:129]
+        attended[j] = jnp.concatenate([first, second], axis=0).T.astype(bf16)
         return carry
 
-    lax.fori_loop(0, pairs, pair, 0)
+    lax.fori_loop(0, pairs, pair, 0, unroll=True)
     joined = jnp.concatenate([attended[j] for j in range(pairs)], axis=1)
     spaced = stepped_ref[...] + dot(joined, out_ref[...])
     spaced_ref[...] = spaced
@@ -222,9 +223,9 @@
         in_specs=[vmem()] * 6,
         out_specs=[vmem()] * 2,
         scratch_shapes=[
-            pltpu.VMEM((pairs, rows, 128), bf16),
+            pltpu.VMEM((pairs, 128, rows), bf16),
             pltpu.VMEM((pairs, 4 * rows, 128), bf16),
-            pltpu.VMEM((pairs, 4 * rows, 256), bf16),
+            pltpu.VMEM((pairs, 144, 2 * rows), bf16),
             pltpu.VMEM((pairs, rows, 128), bf16),
         ],
         compiler_params=params(40),
@@ -233,7 +234,7 @@
     )(own, peer, stepped, qkv, out, norm)
 
 
-def time_kernel_body(x_ref, qkv_ref, o_ref, packed_ref, attended):
+def time_kernel_body(x_ref, qkv_ref, o_ref, packed_ref, turned, attended):
     frames, pixels, channels = x_ref.shape
     rows = frames * pixels
     pairs = channels // 128
@@ -241,25 +242,29 @@
     j = lax.broadcasted_iota(jnp.int32, (rows, rows), 1)
     order = (j == (i % frames) * pixels + i // frames).astype(f32).astype(bf16)
     sorted_rows = dot(order, x_ref[...].reshape(rows, channels)).astype(bf16)
-    packed_ref[...] = dot(sorted_rows, qkv_ref[...]).astype(bf16)
+    packed = dot(sorted_rows, qkv_ref[...]).astype(bf16)
+    packed_ref[...] = packed
+    turned[...] = packed[:, channels : 2 * channels].T
     factor = 64 ** (-0.5) * LOG2E
-    even, odd = half_masks((frames, 128))
-    left = lax.broadcasted_iota(jnp.int32, (frames, 128), 1) < 64
-    low = jnp.full((frames, 128), -jnp.inf, f32)
-
-    def pixel(p, carry):
-        at = pl.multiple_of(p * frames, frames)
+    even, odd = half_masks((128, 128))
+    above = lax.broadcasted_iota(jnp.int32, (128, 128), 0) < 64
+    left = lax.broadcasted_iota(jnp.int32, (128, 128), 1) < 64
+    same = above == left
+    zero = jnp.zeros((128, 128), bf16)
+
+    def two_pixels(at):
         for j in range(pairs):
-            q = packed_ref[pl.ds(at, frames), j * 128 : j * 128 + 128]
-            k = packed_ref[pl.ds(at, frames), channels + j * 128 : channels + j * 128 + 128]
-            v = packed_ref[
-                pl.ds(at, frames), 2 * channels + j * 128 : 2 * channels + j * 128 + 128
-            ]
-            scores = dot(q, jnp.concatenate([k * even, k * odd], axis=0), ((1,), (1,)))
-            top_even = jnp.max(jnp.where(left, scores, low), axis=-1, keepdims=True)
-            top_odd = jnp.max(jnp.where(left, low, scores), axis=-1, keepdims=True)
-            top = jnp.where(left, top_even, top_odd)
-            weights = jnp.exp2((scores - top) * factor).astype(bf16)
+            lanes = slice(j * 128, j * 128 + 128)
+            q = packed_ref[at, lanes]
+            v = packed_ref[at, 2 * channels + j * 128 : 2 * channels + j * 128 + 128]
+            k = turned[lanes, at]
+            keys = jnp.concatenate([jnp.where(above, k, zero), jnp.where(above, zero, k)], axis=1)
+            scores = dot(q, keys)
+            parts = []
+            for part in range(2):
+                own = jnp.where(same, scores[:, part * 128 : part * 128 + 128], -jnp.inf)
+                top = jnp.max(own, axis=-1, keepdims=True)
+                parts.append(jnp.exp2((own - top) * factor).astype(bf16))
             both = jnp.concatenate(
                 [
                     jnp.concatenate([v * even, even], axis=1),
@@ -267,13 +272,11 @@
                 ],
                 axis=0,
             )
-            found = dot(weights, both)
-            attended[pl.ds(at, frames), j * 128 : j * 128 + 128] = (
-                found[:, :128] / found[:, 128:]
-            ).astype(bf16)
-        return carry
-
-    lax.fori_loop(0, pixels, pixel, 0)
+            found = dot(jnp.concatenate(parts, axis=1), both)
+            attended[at, lanes] = (found[:, :128] / found[:, 128:]).astype(bf16)
+
+    for p in range(pixels // 2):
+        two_pixels(slice(p * 128, p * 128 + 128))
     back = dot(order, attended[...], ((0,), (0,))).astype(bf16)
     o_ref[...] = back.reshape(frames, pixels, channels)
 
@@ -288,6 +291,7 @@
         out_specs=vmem(),
         scratch_shapes=[
             pltpu.VMEM((rows, 3 * channels), bf16),
+            pltpu.VMEM((channels, rows), bf16),
             pltpu.VMEM((rows, channels), bf16),
         ],
         compiler_params=params(32),

time: 184 us -> 169 us (0.918)
  Pallas kernels: 37.7 us -> 22.2 us
    pallas_call x1, Pallas kernels: 13.4 us -> 3.79 us  [time_attend(): pl.pallas_call(time_kernel_body, out_shape=jax.ShapeDtypeStruct(x.shape,...]
    pallas_call x1, Pallas kernels: 16.2 us -> 10.4 us  [space(): pl.pallas_call(space_kernel, out_shape=[jax.ShapeDtypeStruct((rows, chann...]
where the time goes in v2:
time: 169 us
  blocking collectives  89 us (53%)
  starting transfers between devices  39.6 us (23%)
  Pallas kernels  22.2 us (13%)
  waiting for transfers between devices  12.2 us (7%)
  local copies, waits for them, and re-layouts  5.27 us (3%)
    all_to_all x1, blocking collectives, body(): lax.all_to_all(normed.reshape(count, pixels // count, channels), FRAME, s...  45.1 us
    all_to_all x1, blocking collectives, body(): lax.all_to_all(result, FRAME, split_axis=0, concat_axis=0, tiled=True)  43.9 us
    ppermute x1, starting transfers between devices, body(): high = lax.ppermute(mine, FRAME, backward)  24.4 us
    all_to_all x1, starting transfers between devices, body(): lax.all_to_all(sums, FRAME_ROW, split_axis=0, concat_axis=0, tiled=True)  12.9 us
    pallas_call x1, Pallas kernels, space(): pl.pallas_call(space_kernel, out_shape=[jax.ShapeDtypeStruct((rows, chann...  10.4 us
    all_to_all x1, waiting for transfers between devices, body(): lax.all_to_all(sums, FRAME_ROW, split_axis=0, concat_axis=0, tiled=True)  10.2 us
    pallas_call x1, Pallas kernels, front(): pl.pallas_call(functools.partial(front_kernel, number), out_shape=[jax.Sh...  4.04 us
    unnamed x16, local copies, waits for them, and re-layouts  3.89 us
  transfers between devices with their start and end apart: 4, of which 2 were waited for; matrix products, arithmetic and copies ran while one was open for 1% of the time, Pallas kernels for 1%

profile of v2, /device:TPU:38, one launch (start us, length us, event | category | flops | bytes accessed | tf_op | source)
XLA Modules:
  0.0 168.6 jit_solution(13223115917010878555)
XLA Ops:
  0.0 24.4 %collective-permute-start.1 = (bf16[512,640]{1,0:T(8,128)(2,1)}, bf16[512,640]{1,0:T(8,128)(2,1)S(1)}, u32[]{:S(2)}, u32[]{:S(2)}) collective-permute-start(bf16[512,640]{1,0:T(8,128)(2,1)} %bitcast.7), channel_id=1, source_target_pairs={{2,0},{4,2},{6,4},{8,6},{10,8},{12,10},{14,12},{16,14},{18,16},{20... | collective-permute-start | bytes 1966088 | tf_op jit(solution)/shard_map/ppermute | solution.py:334
  24.4 2.0 %collective-permute-start = (bf16[512,640]{1,0:T(8,128)(2,1)}, bf16[512,640]{1,0:T(8,128)(2,1)S(1)}, u32[]{:S(2)}, u32[]{:S(2)}) collective-permute-start(bf16[512,640]{1,0:T(8,128)(2,1)} %bitcast.8), channel_id=1, source_target_pairs={{0,2},{2,4},{4,6},{6,8},{8,10},{10,12},{12,14},{14,16},{16,18},{18... | collective-permute-start | bytes 1966088 | tf_op jit(solution)/shard_map/ppermute | solution.py:333
  26.4 0.0 copy-start.1
  26.4 1.1 copy-done.1
  27.5 0.0 copy-start.6
  27.5 1.7 group_sums.1
  29.2 0.0 copy-start.7
  29.2 12.9 %all-to-all-start = ((f32[128,1,128]{2,1,0:T(1,128)}), f32[128,1,128]{2,1,0:T(1,128)S(1)}, u32[]{:S(2)}, u32[]{:S(2)}) async-start(f32[128,1,128]{2,1,0:T(1,128)} %group_sums.1), calls=%async_computation | async-start | bytes 131072 | tf_op jit(solution)/shard_map/all_to_all | solution.py:337
  42.1 0.7 reshape.22.gain_ref
  42.8 0.7 reshape.23.norm_ref
  43.5 0.1 add_convert_fusion.edge_ref
  43.6 10.2 %all-to-all-done.sums_ref = f32[128,1,128]{2,1,0:T(1,128)S(1)} async-done(((f32[128,1,128]{2,1,0:T(1,128)}), f32[128,1,128]{2,1,0:T(1,128)S(1)}, u32[]{:S(2)}, u32[]{:S(2)}) %all-to-all-start) | async-done | bytes 65568 | tf_op jit(solution)/shard_map/all_to_all | solution.py:337
  53.7 0.0 collective-permute-done.1.high_ref
  53.7 0.0 collective-permute-done.low_ref
  53.8 0.0 copy-start.2
  53.8 1.1 copy-done.2
  54.8 0.0 copy-start.3
  54.8 1.7 %copy-done.3 = bf16[3,640,640]{2,1,0:T(8,128)(2,1)S(1)} copy-done((bf16[3,640,640]{2,1,0:T(8,128)(2,1)S(1)}, bf16[3,640,640]{2,1,0:T(8,128)(2,1)}, u32[]{:S(2)}) %copy-start.3) | copy-done | bytes 2457624
  56.5 0.0 copy-start.4
  56.5 4.0 %front.1 = (f32[512,640]{1,0:T(8,128)S(1)}, bf16[512,640]{1,0:T(8,128)(2,1)S(1)}) custom-call(s32[2]{0:T(128)S(1)} %add_convert_fusion.edge_ref, f32[128,1,128]{2,1,0:T(1,128)S(1)} %all-to-all-done.sums_ref, f32[1,640]{1,0:T(1,128)S(1)} %reshape.22.gain_ref, bf16[512,640]{1,0:T(8,128)(2,1)S(1)} %collective-permute-done.low_ref, ...), custom_call_target="tpu_custom_call" | custom-call | flops 1258291200 | bytes 4587520 | tf_op jit(solution)/shard_map/front/pallas_call | solution.py:136
  60.6 0.3 collective-permute-start.2
  60.9 0.0 copy-done.7
  60.9 2.0 %collective-permute-done.2.peer_ref = bf16[512,640]{1,0:T(8,128)(2,1)S(1)} collective-permute-done((bf16[512,640]{1,0:T(8,128)(2,1)S(1)}, bf16[512,640]{1,0:T(8,128)(2,1)S(1)}, u32[]{:S(2)}, u32[]{:S(2)}) %collective-permute-start.2) | collective-permute-done | bytes 655392 | tf_op jit(solution)/shard_map/ppermute | solution.py:345
  63.0 0.0 copy-done.6
  63.0 0.0 copy-done.4
  63.0 0.0 copy-start.5
  63.0 10.4 %space.1 = (f32[512,640]{1,0:T(8,128)S(1)}, bf16[512,640]{1,0:T(8,128)(2,1)S(1)}) custom-call(bf16[512,640]{1,0:T(8,128)(2,1)S(1)} %get-tuple-element.9.own_ref, bf16[512,640]{1,0:T(8,128)(2,1)S(1)} %collective-permute-done.2.peer_ref, f32[512,640]{1,0:T(8,128)S(1)} %get-tuple-element.10.stepped_ref, bf16[640,1920]{1,0:T(8,128)(2,1)S(1)} %copy-done.4, ...), custom_call_target="tpu_custom_call" | custom-call | flops 3858759680 | bytes 4587520 | tf_op jit(solution)/shard_map/space/pallas_call | solution.py:217
  73.4 45.1 %all_to_all.15.x_ref = bf16[64,8,640]{2,1,0:T(8,128)(2,1)S(1)} all-to-all(bf16[64,8,640]{2,1,0:T(8,128)(2,1)S(1)} %bitcast.11), channel_id=1, replica_groups=mesh['groups'=2,'frame'=64,'row'=2] {'frame'}, dimensions={0} | all-to-all | bytes 1310720 | tf_op jit(solution)/shard_map/all_to_all | solution.py:347
  118.5 0.0 copy-done.5
  118.5 0.0 copy-start
  118.5 3.8 %time_attend.1 = bf16[64,8,640]{2,1,0:T(8,128)(2,1)S(1)} custom-call(bf16[64,8,640]{2,1,0:T(8,128)(2,1)S(1)} %all_to_all.15.x_ref, bf16[640,1920]{1,0:T(8,128)(2,1)S(1)} %copy-done.5), custom_call_target="tpu_custom_call" | custom-call | flops 1929379840 | bytes 1310720 | tf_op jit(solution)/shard_map/time_attend/pallas_call | solution.py:287
  122.3 43.9 %all_to_all.16 = bf16[64,8,640]{2,1,0:T(8,128)(2,1)S(1)} all-to-all(bf16[64,8,640]{2,1,0:T(8,128)(2,1)S(1)} %time_attend.1), channel_id=1, replica_groups=mesh['groups'=2,'frame'=64,'row'=2] {'frame'}, dimensions={0} | all-to-all | bytes 1310720 | tf_op jit(solution)/shard_map/all_to_all | solution.py:352
  166.2 0.0 copy-done
  166.2 2.4 %finish.1 = f32[512,640]{1,0:T(8,128)} custom-call(f32[512,640]{1,0:T(8,128)S(1)} %get-tuple-element.11.base_ref, bf16[512,640]{1,0:T(8,128)(2,1)S(1)} %bitcast.6, bf16[640,640]{1,0:T(8,128)(2,1)S(1)} %copy-done), custom_call_target="tpu_custom_call" | custom-call | flops 419430400 | bytes 3276800 | tf_op jit(solution)/shard_map/finish/pallas_call | solution.py:311
  (1 shorter events, 0.0 us)
Async XLA Ops:
  0.0 53.7 %collective-permute-start.1 = (bf16[512,640]{1,0:T(8,128)(2,1)}, bf16[512,640]{1,0:T(8,128)(2,1)S(1)}, u32[]{:S(2)}, u32[]{:S(2)}) collective-permute-start(bf16[512,640]{1,0:T(8,128)(2,1)} %bitcast.7), channel_id=1, source_target_pairs={{2,0},{4,2},{6,4},{8,6},{10,8},{12,10},{14,12},{16,14},{18,16},{20... | collective-permute-start | bytes 1966088 | tf_op jit(solution)/shard_map/ppermute | solution.py:334
  24.4 29.3 %collective-permute-start = (bf16[512,640]{1,0:T(8,128)(2,1)}, bf16[512,640]{1,0:T(8,128)(2,1)S(1)}, u32[]{:S(2)}, u32[]{:S(2)}) collective-permute-start(bf16[512,640]{1,0:T(8,128)(2,1)} %bitcast.8), channel_id=1, source_target_pairs={{0,2},{2,4},{4,6},{6,8},{8,10},{10,12},{12,14},{14,16},{16,18},{18... | collective-permute-start | bytes 1966088 | tf_op jit(solution)/shard_map/ppermute | solution.py:333
  26.4 1.1 copy-start.1
  27.5 35.5 %copy-start.6 = (bf16[640,640]{1,0:T(8,128)(2,1)S(1)}, bf16[640,640]{1,0:T(8,128)(2,1)}, u32[]{:S(2)}) copy-start(bf16[640,640]{1,0:T(8,128)(2,1)} %out_ref.1) | copy-start | bytes 2457604
  29.2 31.8 %copy-start.7 = (f32[640]{0:T(1024)S(1)}, f32[640]{0:T(1024)}, u32[]{:S(2)}) copy-start(f32[640]{0:T(1024)} %param.15) | copy-start | bytes 7684
  29.2 24.6 %all-to-all-start = ((f32[128,1,128]{2,1,0:T(1,128)}), f32[128,1,128]{2,1,0:T(1,128)S(1)}, u32[]{:S(2)}, u32[]{:S(2)}) async-start(f32[128,1,128]{2,1,0:T(1,128)} %group_sums.1), calls=%async_computation | async-start | bytes 131072 | tf_op jit(solution)/shard_map/all_to_all | solution.py:337
  53.8 1.1 copy-start.2
  54.8 1.7 %copy-start.3 = (bf16[3,640,640]{2,1,0:T(8,128)(2,1)S(1)}, bf16[3,640,640]{2,1,0:T(8,128)(2,1)}, u32[]{:S(2)}) copy-start(bf16[3,640,640]{2,1,0:T(8,128)(2,1)} %kernel_ref.1) | copy-start | bytes 7372804
  56.5 6.5 %copy-start.4 = (bf16[640,1920]{1,0:T(8,128)(2,1)S(1)}, bf16[640,1920]{1,0:T(8,128)(2,1)}, u32[]{:S(2)}) copy-start(bf16[640,1920]{1,0:T(8,128)(2,1)} %qkv_ref.2) | copy-start | bytes 7372804
  60.6 2.4 %collective-permute-start.2 = (bf16[512,640]{1,0:T(8,128)(2,1)S(1)}, bf16[512,640]{1,0:T(8,128)(2,1)S(1)}, u32[]{:S(2)}, u32[]{:S(2)}) collective-permute-start(bf16[512,640]{1,0:T(8,128)(2,1)S(1)} %get-tuple-element.9.own_ref), channel_id=1, source_target_pairs={{0,1},{1,0},{2,3},{3,2},{4,5},{5,4},{6,7},{7,6},{8,9},{9,8},{10,11... | collective-permute-start | bytes 1966088 | tf_op jit(solution)/shard_map/ppermute | solution.py:345
  63.0 55.5 %copy-start.5 = (bf16[640,1920]{1,0:T(8,128)(2,1)S(1)}, bf16[640,1920]{1,0:T(8,128)(2,1)}, u32[]{:S(2)}) copy-start(bf16[640,1920]{1,0:T(8,128)(2,1)} %qkv_ref.3) | copy-start | bytes 7372804
  118.5 47.7 %copy-start = (bf16[640,640]{1,0:T(8,128)(2,1)S(1)}, bf16[640,640]{1,0:T(8,128)(2,1)}, u32[]{:S(2)}) copy-start(bf16[640,640]{1,0:T(8,128)(2,1)} %w_ref.1) | copy-start | bytes 2457604

commit v3 on v2

--- a/solution.py
+++ b/solution.py
@@ -52,56 +52,61 @@
     return (shifted * lax.rsqrt(spread + epsilon) * gain).astype(bf16)
 
 
-def sums_kernel(x_ref, o_ref, acc):
-    step = pl.program_id(0)
-    x = x_ref[...].astype(f32)
-    rows, channels = x.shape
-    part = x.reshape(rows // 8, 8, channels)
-    first, second = jnp.sum(part, axis=0), jnp.sum(part * part, axis=0)
-
-    @pl.when(step == 0)
-    def _():
-        acc[0] = first
-        acc[1] = second
-
-    @pl.when(step > 0)
-    def _():
-        acc[0] += first
-        acc[1] += second
-
-    @pl.when(step == pl.num_programs(0) - 1)
-    def _():
-        exact = lax.Precision.HIGHEST
-        total = dot(acc[0], group_slots(channels, 0), ((1,), (1,)), exact)
-        total += dot(acc[1], group_slots(channels, GROUPS), ((1,), (1,)), exact)
-        row = jnp.sum(total, axis=0, keepdims=True)
-        o_ref[...] = jnp.broadcast_to(row[None], o_ref.shape)
+def sums_kernel(x_ref, o_ref, near, sem):
+    rows, channels = x_ref.shape
+    parts = 4
+    tile = rows // parts
+    copies = [
+        pltpu.make_async_copy(
+            x_ref.at[i * tile : i * tile + tile], near.at[i * tile : i * tile + tile], sem.at[i]
+        )
+        for i in range(parts)
+    ]
+    for copy in copies:
+        copy.start()
+    first = jnp.zeros((8, channels), f32)
+    second = jnp.zeros((8, channels), f32)
+    slots, later = group_slots(channels, 0), group_slots(channels, GROUPS)
+    for i, copy in enumerate(copies):
+        copy.wait()
+        x = near[i * tile : i * tile + tile].astype(f32).reshape(tile // 8, 8, channels)
+        first += jnp.sum(x, axis=0)
+        second += jnp.sum(x * x, axis=0)
+    exact = lax.Precision.HIGHEST
+    total = dot(first, slots, ((1,), (1,)), exact) + dot(second, later, ((1,), (1,)), exact)
+    row = jnp.sum(total, axis=0, keepdims=True)
+    o_ref[...] = jnp.broadcast_to(row[None], o_ref.shape)
 
 
 def group_sums(latent, members):
     rows, channels = latent.shape
-    tile = rows // 2
     return pl.pallas_call(
         sums_kernel,
         out_shape=jax.ShapeDtypeStruct((members, 1, 128), f32),
-        grid=(rows // tile,),
-        in_specs=[pl.BlockSpec((tile, channels), lambda i: (i, 0))],
-        out_specs=pl.BlockSpec((members, 1, 128), lambda i: (0, 0, 0)),
-        scratch_shapes=[pltpu.VMEM((2, 8, channels), f32)],
+        in_specs=[pl.BlockSpec(memory_space=pltpu.HBM)],
+        out_specs=vmem(),
+        scratch_shapes=[pltpu.VMEM((rows, channels), bf16), pltpu.SemaphoreType.DMA((4,))],
         compiler_params=params(16),
         cost_estimate=cost(4 * rows * channels, 2 * rows * channels),
         name="group_sums",
-    )(latent)
+    )(pin(latent))
+
+
+def pin(x):
+    return pltpu.with_memory_space_constraint(x, pltpu.HBM)
 
 
 def front_kernel(
-    number, edge_ref, sums_ref, gain_ref, low_ref, mid_ref, high_ref, kernel_ref, norm_ref,
-    stepped_ref, tokens_ref, scale
+    number, edge_ref, sums_ref, gain_ref, low_ref, mid_ref, high_ref, kernel_far, norm_ref,
+    stepped_ref, tokens_ref, scale, kernel_ref, sem
 ):
     channels = mid_ref.shape[1]
-
-    @pl.when(pl.program_id(0) == 0)
+    first_step = pl.program_id(0) == 0
+    get_kernel = pltpu.make_async_copy(kernel_far, kernel_ref, sem)
+
+    @pl.when(first_step)
     def _():
+        get_kernel.start()
         exact = lax.Precision.HIGHEST
         total = jnp.broadcast_to(jnp.sum(sums_ref[...], axis=0), (8, 128))
         center = dot(total, group_slots(channels, 0), precision=exact) / number
@@ -109,6 +114,7 @@
         scaling = lax.rsqrt(square - center * center + epsilon) * gain_ref[...]
         scale[0] = scaling
         scale[1] = center
+        get_kernel.wait()
 
     scaling, center = scale[0, 0:1], scale[1, 0:1]
 
@@ -147,15 +153,19 @@
             block,
             block,
             block,
-            vmem(),
+            pl.BlockSpec(memory_space=pltpu.HBM),
             one,
         ],
         out_specs=[block, block],
-        scratch_shapes=[pltpu.VMEM((2, 8, channels), f32)],
+        scratch_shapes=[
+            pltpu.VMEM((2, 8, channels), f32),
+            pltpu.VMEM(time_kernel.shape, bf16),
+            pltpu.SemaphoreType.DMA,
+        ],
         compiler_params=params(24),
         cost_estimate=cost(6 * rows * channels * channels, 14 * rows * channels),
         name="front",
-    )(edge, sums, gain, low, mid, high, time_kernel, norm)
+    )(edge, sums, gain, low, pin(mid), high, pin(time_kernel), norm)
 
 
 def half_masks(shape):
@@ -165,73 +175,97 @@
     return even, odd
 
 
+def split_heads(packed, keys, values, at=0):
+    rows, width = packed.shape
+    channels = width // 2
+    even, odd = half_masks((rows, 128))
+    for j in range(channels // 128):
+        k = packed[:, j * 128 : j * 128 + 128]
+        v = packed[:, channels + j * 128 : channels + j * 128 + 128].T
+        keys[j, 0, at : at + rows] = k * even
+        keys[j, 1, at : at + rows] = k * odd
+        values[j, :128, at : at + rows] = v
+        values[j, 128:, at : at + rows] = jnp.ones((16, rows), bf16)
+
+
+def project_kernel(own_ref, qkv_ref, queries, keys, values):
+    channels = own_ref.shape[1]
+    own = own_ref[...]
+    packed = dot(own, qkv_ref[:, :channels]).astype(bf16)
+    for j in range(channels // 128):
+        queries[j] = packed[:, j * 128 : j * 128 + 128].T
+    split_heads(dot(own, qkv_ref[:, channels:]).astype(bf16), keys, values)
+
+
+def kept(rows, channels):
+    pairs = channels // 128
+    return [(pairs, 128, rows), (pairs, 2, rows, 128), (pairs, 144, rows)]
+
+
+def project(own, qkv):
+    rows, channels = own.shape
+    return pl.pallas_call(
+        project_kernel,
+        out_shape=[jax.ShapeDtypeStruct(shape, bf16) for shape in kept(rows, channels)],
+        in_specs=[vmem()] * 2,
+        out_specs=[vmem()] * 3,
+        compiler_params=params(20),
+        cost_estimate=cost(6 * rows * channels * channels, 8 * rows * channels),
+        name="project",
+    )(own, qkv)
+
+
 def space_kernel(
-    own_ref, peer_ref, stepped_ref, qkv_ref, out_ref, norm_ref, spaced_ref, normed_ref,
-    queries, keys, values, attended
+    queries, near_keys, near_values, peer_ref, stepped_ref, qkv_ref, out_ref, norm_ref,
+    spaced_ref, normed_ref, keys, values, attended
 ):
-    rows, channels = own_ref.shape
+    rows, channels = peer_ref.shape
     pairs = channels // 128
-    length = 2 * rows
-    even, odd = half_masks((rows, 128))
-    for half, ref in enumerate((own_ref, peer_ref)):
-        packed = dot(ref[...], qkv_ref[:, channels:]).astype(bf16)
-        at = half * rows
-        for j in range(pairs):
-            k = packed[:, j * 128 : j * 128 + 128]
-            keys[j, at : at + rows] = k * even
-            keys[j, length + at : length + at + rows] = k * odd
-            v = packed[:, channels + j * 128 : channels + j * 128 + 128].T
-            values[j, :128, at : at + rows] = v
-            values[j, 128:, at : at + rows] = jnp.ones((16, rows), bf16)
-    packed = dot(own_ref[...], qkv_ref[:, :channels]).astype(bf16)
+    keys[:, :, :rows] = near_keys[...]
+    values[:, :, :rows] = near_values[...]
+    split_heads(dot(peer_ref[...], qkv_ref[:, channels:]).astype(bf16), keys, values, rows)
+    factor = 64 ** (-0.5) * LOG2E
     for j in range(pairs):
-        queries[j] = packed[:, j * 128 : j * 128 + 128].T
-
-    factor = 64 ** (-0.5) * LOG2E
-
-    def pair(j, carry):
         q = queries[j]
-        weights = []
+        parts, weights = [], []
         for part in range(2):
-            low = part * length
-            scores = dot(keys[j, low : low + length], q)
+            scores = dot(keys[j, part], q)
             top = jnp.max(scores, axis=0, keepdims=True)
             weights.append(jnp.exp2((scores - top) * factor).astype(bf16))
-        first = dot(values[j], weights[0])
-        second = dot(values[j], weights[1])
-        first = first[:64] / first[128:129]
-        second = second[64:128] / second[128:129]
-        attended[j] = jnp.concatenate([first, second], axis=0).T.astype(bf16)
-        return carry
-
-    lax.fori_loop(0, pairs, pair, 0, unroll=True)
+        for part in range(2):
+            found = dot(values[j], weights[part])
+            parts.append(found[part * 64 : part * 64 + 64] / found[128:129])
+        attended[j] = jnp.concatenate(parts, axis=0).T.astype(bf16)
     joined = jnp.concatenate([attended[j] for j in range(pairs)], axis=1)
     spaced = stepped_ref[...] + dot(joined, out_ref[...])
     spaced_ref[...] = spaced
     normed_ref[...] = layer_norm(spaced, norm_ref[...])
 
 
-def space(own, peer, stepped, qkv, out, norm):
-    rows, channels = own.shape
-    pairs = channels // 128
+def space(projected, peer, stepped, qkv, out, norm):
+    rows, channels = peer.shape
+    _, keys, values = kept(2 * rows, channels)
     return pl.pallas_call(
         space_kernel,
         out_shape=[
             jax.ShapeDtypeStruct((rows, channels), f32),
             jax.ShapeDtypeStruct((rows, channels), bf16),
         ],
-        in_specs=[vmem()] * 6,
+        in_specs=[vmem()] * 8,
         out_specs=[vmem()] * 2,
         scratch_shapes=[
-            pltpu.VMEM((pairs, 128, rows), bf16),
-            pltpu.VMEM((pairs, 4 * rows, 128), bf16),
-            pltpu.VMEM((pairs, 144, 2 * rows), bf16),
-            pltpu.VMEM((pairs, rows, 128), bf16),
-        ],
-        compiler_params=params(40),
-        cost_estimate=cost(12 * rows * channels * channels + 8 * rows * rows * channels, 14 * rows * channels, 2 * HEADS * rows * rows),
+            pltpu.VMEM(keys, bf16),
+            pltpu.VMEM(values, bf16),
+            pltpu.VMEM((channels // 128, rows, 128), bf16),
+        ],
+        compiler_params=params(36),
+        cost_estimate=cost(
+            6 * rows * channels * channels + 8 * rows * rows * channels,
+            14 * rows * channels,
+            2 * HEADS * rows * rows,
+        ),
         name="space",
-    )(own, peer, stepped, qkv, out, norm)
+    )(*projected, peer, stepped, qkv, out, norm)
 
 
 def time_kernel_body(x_ref, qkv_ref, o_ref, packed_ref, turned, attended):
@@ -306,7 +340,7 @@
 
 def finish(base, x, w):
     rows, channels = base.shape
-    tile = rows // 4
+    tile = rows // 2
     block = pl.BlockSpec((tile, channels), lambda i: (i, 0))
     return pl.pallas_call(
         finish_kernel,
@@ -333,8 +367,9 @@
     low = lax.ppermute(mine, FRAME, forward)
     high = lax.ppermute(mine, FRAME, backward)
     members = lax.axis_size(FRAME_ROW)
-    sums = group_sums(mine, members)
-    sums = lax.all_to_all(sums, FRAME_ROW, split_axis=0, concat_axis=0, tiled=True)
+    sums = group_sums(mine, count)
+    sums += lax.ppermute(sums, "row", [(0, 1), (1, 0)])
+    sums = lax.all_to_all(sums, FRAME, split_axis=0, concat_axis=0, tiled=True)
     number = float(members * pixels * (channels // GROUPS))
     here = lax.axis_index(FRAME)
     edge = jnp.stack([here > 0, here < count - 1]).astype(jnp.int32)
@@ -343,7 +378,8 @@
         space_norm.reshape(1, -1), number,
     )
     peer = lax.ppermute(tokens, "row", [(0, 1), (1, 0)])
-    spaced, normed = space(tokens, peer, stepped, space_qkv, space_out, time_norm.reshape(1, -1))
+    projected = project(tokens, space_qkv)
+    spaced, normed = space(projected, peer, stepped, space_qkv, space_out, time_norm.reshape(1, -1))
     moved = lax.all_to_all(
         normed.reshape(count, pixels // count, channels),
         FRAME, split_axis=0, concat_axis=0, tiled=True,

time: 169 us -> 164 us (0.970)
  local copies, waits for them, and re-layouts: 5.27 us -> 1.41 us
  starting transfers between devices: 39.6 us -> 36.8 us
  Pallas kernels: 22.2 us -> 24.3 us
    unnamed x16 -> x10, local copies, waits for them, and re-layouts: 3.89 us -> 0.02 us
    all_to_all x1, starting transfers between devices: 12.9 us -> 9.99 us  [body(): sums = lax.all_to_all(sums, FRAME, split_axis=0, concat_axis=0, tiled=True)]
    ppermute x1, waiting for transfers between devices: 2.05 us -> 0.12 us  [body(): peer = lax.ppermute(tokens, 'row', [(0, 1), (1, 0)])]
    pallas_call x0 -> x1, Pallas kernels: none -> 1.9 us  [project(): pl.pallas_call(project_kernel, out_shape=[jax.ShapeDtypeStruct(shape, bf1...]
  transfers between devices with their start and end apart: 4 -> 5, of which waited for: 2 -> 3; matrix products, arithmetic and copies ran while one was open for 1% -> 1% of each run, Pallas kernels for 1% -> 2%
where the time goes in v3:
time: 164 us; the launch traced here: 163 us
  blocking collectives  88.1 us (54%)
  starting transfers between devices  36.8 us (22%)
  Pallas kernels  24.3 us (15%)
  waiting for transfers between devices  11.7 us (7%)
    all_to_all x1, blocking collectives, body(): lax.all_to_all(normed.reshape(count, pixels // count, channels), FRAME, s...  44.4 us
    all_to_all x1, blocking collectives, body(): lax.all_to_all(result, FRAME, split_axis=0, concat_axis=0, tiled=True)  43.7 us
    ppermute x1, starting transfers between devices, body(): high = lax.ppermute(mine, FRAME, backward)  24.4 us
    all_to_all x1, waiting for transfers between devices, body(): sums = lax.all_to_all(sums, FRAME, split_axis=0, concat_axis=0, tiled=True)  10.4 us
    all_to_all x1, starting transfers between devices, body(): sums = lax.all_to_all(sums, FRAME, split_axis=0, concat_axis=0, tiled=True)  9.99 us
    pallas_call x1, Pallas kernels, space(): pl.pallas_call(space_kernel, out_shape=[jax.ShapeDtypeStruct((rows, chann...  9.28 us
    pallas_call x1, Pallas kernels, front(): pl.pallas_call(functools.partial(front_kernel, number), out_shape=[jax.Sh...  5.64 us
    pallas_call x1, Pallas kernels, time_attend(): pl.pallas_call(time_kernel_body, out_shape=jax.ShapeDtypeStruct(x.shape,...  3.78 us
  transfers between devices with their start and end apart: 5, of which 3 were waited for; matrix products, arithmetic and copies ran while one was open for 1% of the time, Pallas kernels for 2%

profile of v3, /device:TPU:38, one launch (start us, length us, event | category | flops | bytes accessed | tf_op | source)
XLA Modules:
  0.0 163.2 jit_solution(14425294862966243124)
XLA Ops:
  0.0 24.4 %collective-permute-start.2 = (bf16[512,640]{1,0:T(8,128)(2,1)}, bf16[512,640]{1,0:T(8,128)(2,1)S(1)}, u32[]{:S(2)}, u32[]{:S(2)}) collective-permute-start(bf16[512,640]{1,0:T(8,128)(2,1)} %bitcast.8), channel_id=1, source_target_pairs={{2,0},{4,2},{6,4},{8,6},{10,8},{12,10},{14,12},{16,14},{18,16},{20... | collective-permute-start | bytes 1966088 | tf_op jit(solution)/shard_map/ppermute | solution.py:368
  24.4 2.0 %collective-permute-start.1 = (bf16[512,640]{1,0:T(8,128)(2,1)}, bf16[512,640]{1,0:T(8,128)(2,1)}, u32[]{:S(2)}, u32[]{:S(2)}) collective-permute-start(bf16[512,640]{1,0:T(8,128)(2,1)} %bitcast.9), channel_id=1, source_target_pairs={{0,2},{2,4},{4,6},{6,8},{8,10},{10,12},{12,14},{14,16},{16,18},{18... | collective-permute-start | bytes 1966088 | tf_op jit(solution)/shard_map/ppermute | solution.py:367
  26.4 2.0 %group_sums.1 = f32[64,1,128]{2,1,0:T(1,128)S(1)} custom-call(bf16[512,640]{1,0:T(8,128)(2,1)} %bitcast.10), custom_call_target="tpu_custom_call" | custom-call | flops 1310720 | bytes 655360 | tf_op jit(solution)/shard_map/group_sums/pallas_call | solution.py:83
  28.4 0.1 collective-permute-start
  28.5 1.2 collective-permute-done
  29.7 0.6 add.3
  30.3 10.0 %all-to-all-start = ((f32[64,1,128]{2,1,0:T(1,128)}), f32[64,1,128]{2,1,0:T(1,128)S(1)}, u32[]{:S(2)}, u32[]{:S(2)}) async-start(f32[64,1,128]{2,1,0:T(1,128)} %add.3), calls=%async_computation | async-start | bytes 65536 | tf_op jit(solution)/shard_map/all_to_all | solution.py:372
  40.4 0.7 reshape.22.gain_ref
  41.0 0.7 reshape.23.norm_ref
  41.7 0.1 add_convert_fusion.edge_ref
  41.8 0.0 copy-start.4
  41.8 0.0 copy-start.1
  41.8 10.4 %all-to-all-done.sums_ref = f32[64,1,128]{2,1,0:T(1,128)S(1)} async-done(((f32[64,1,128]{2,1,0:T(1,128)}), f32[64,1,128]{2,1,0:T(1,128)S(1)}, u32[]{:S(2)}, u32[]{:S(2)}) %all-to-all-start) | async-done | bytes 32800 | tf_op jit(solution)/shard_map/all_to_all | solution.py:372
  52.2 0.0 collective-permute-done.2.high_ref
  52.2 0.0 collective-permute-done.1.low_ref
  52.2 5.6 %front.1 = (f32[512,640]{1,0:T(8,128)S(1)}, bf16[512,640]{1,0:T(8,128)(2,1)S(1)}) custom-call(s32[2]{0:T(128)S(1)} %add_convert_fusion.edge_ref, f32[64,1,128]{2,1,0:T(1,128)S(1)} %all-to-all-done.sums_ref, f32[1,640]{1,0:T(1,128)S(1)} %reshape.22.gain_ref, bf16[512,640]{1,0:T(8,128)(2,1)} %collective-permute-done.1.low_ref, bf16[512,640]{1,0:T(8,128)(2,1)} %bitcast.11, ...), custom_call_target="tpu_custom_call" | custom-call | flops 1258291200 | bytes 4587520 | tf_op jit(solution)/shard_map/front/pallas_call | solution.py:142
  57.9 0.3 collective-permute-start.3
  58.2 0.0 copy-done.4
  58.2 0.0 copy-done.1
  58.2 0.0 copy-start.3
  58.2 1.9 %project.1 = (bf16[5,128,512]{2,1,0:T(8,128)(2,1)S(1)}, bf16[5,2,512,128]{3,2,1,0:T(8,128)(2,1)S(1)}, bf16[5,144,512]{2,1,0:T(8,128)(2,1)S(1)}) custom-call(bf16[512,640]{1,0:T(8,128)(2,1)S(1)} %get-tuple-element.12.own_ref, bf16[640,1920]{1,0:T(8,128)(2,1)S(1)} %copy-done.1), custom_call_target="tpu_custom_call" | custom-call | flops 1258291200 | bytes 2621440 | tf_op jit(solution)/shard_map/project/pallas_call | solution.py:207
  60.1 0.1 collective-permute-done.3.peer_ref
  60.3 0.0 copy-done.3
  60.3 0.0 copy-start.2
  60.3 9.3 %space.1 = (f32[512,640]{1,0:T(8,128)S(1)}, bf16[512,640]{1,0:T(8,128)(2,1)S(1)}) custom-call(bf16[5,128,512]{2,1,0:T(8,128)(2,1)S(1)} %get-tuple-element.13.queries, bf16[5,2,512,128]{3,2,1,0:T(8,128)(2,1)S(1)} %get-tuple-element.14.near_keys, bf16[5,144,512]{2,1,0:T(8,128)(2,1)S(1)} %get-tuple-element.15.near_values, ...), custom_call_target="tpu_custom_call" | custom-call | flops 2600468480 | bytes 4587520 | tf_op jit(solution)/shard_map/space/pallas_call | solution.py:248
  69.6 44.4 %all_to_all.15.x_ref = bf16[64,8,640]{2,1,0:T(8,128)(2,1)S(1)} all-to-all(bf16[64,8,640]{2,1,0:T(8,128)(2,1)S(1)} %bitcast.7), channel_id=1, replica_groups=mesh['groups'=2,'frame'=64,'row'=2] {'frame'}, dimensions={0} | all-to-all | bytes 1310720 | tf_op jit(solution)/shard_map/all_to_all | solution.py:383
  114.0 0.0 copy-done.2
  114.0 3.8 %time_attend.1 = bf16[64,8,640]{2,1,0:T(8,128)(2,1)S(1)} custom-call(bf16[64,8,640]{2,1,0:T(8,128)(2,1)S(1)} %all_to_all.15.x_ref, bf16[640,1920]{1,0:T(8,128)(2,1)S(1)} %copy-done.2), custom_call_target="tpu_custom_call" | custom-call | flops 1929379840 | bytes 1310720 | tf_op jit(solution)/shard_map/time_attend/pallas_call | solution.py:321
  117.8 0.0 copy-start
  117.8 43.7 %all_to_all.16 = bf16[64,8,640]{2,1,0:T(8,128)(2,1)S(1)} all-to-all(bf16[64,8,640]{2,1,0:T(8,128)(2,1)S(1)} %time_attend.1), channel_id=1, replica_groups=mesh['groups'=2,'frame'=64,'row'=2] {'frame'}, dimensions={0} | all-to-all | bytes 1310720 | tf_op jit(solution)/shard_map/all_to_all | solution.py:388
  161.4 0.0 copy-done
  161.4 1.8 %finish.1 = f32[512,640]{1,0:T(8,128)} custom-call(f32[512,640]{1,0:T(8,128)S(1)} %get-tuple-element.17.base_ref, bf16[512,640]{1,0:T(8,128)(2,1)S(1)} %bitcast.6, bf16[640,640]{1,0:T(8,128)(2,1)S(1)} %copy-done), custom_call_target="tpu_custom_call" | custom-call | flops 419430400 | bytes 3276800 | tf_op jit(solution)/shard_map/finish/pallas_call | solution.py:345
  (1 shorter events, 0.0 us)
Async XLA Ops:
  0.0 52.2 %collective-permute-start.2 = (bf16[512,640]{1,0:T(8,128)(2,1)}, bf16[512,640]{1,0:T(8,128)(2,1)S(1)}, u32[]{:S(2)}, u32[]{:S(2)}) collective-permute-start(bf16[512,640]{1,0:T(8,128)(2,1)} %bitcast.8), channel_id=1, source_target_pairs={{2,0},{4,2},{6,4},{8,6},{10,8},{12,10},{14,12},{16,14},{18,16},{20... | collective-permute-start | bytes 1966088 | tf_op jit(solution)/shard_map/ppermute | solution.py:368
  24.4 27.8 %collective-permute-start.1 = (bf16[512,640]{1,0:T(8,128)(2,1)}, bf16[512,640]{1,0:T(8,128)(2,1)}, u32[]{:S(2)}, u32[]{:S(2)}) collective-permute-start(bf16[512,640]{1,0:T(8,128)(2,1)} %bitcast.9), channel_id=1, source_target_pairs={{0,2},{2,4},{4,6},{6,8},{8,10},{10,12},{12,14},{14,16},{16,18},{18... | collective-permute-start | bytes 1966088 | tf_op jit(solution)/shard_map/ppermute | solution.py:367
  28.4 1.3 collective-permute-start
  30.3 21.9 %all-to-all-start = ((f32[64,1,128]{2,1,0:T(1,128)}), f32[64,1,128]{2,1,0:T(1,128)S(1)}, u32[]{:S(2)}, u32[]{:S(2)}) async-start(f32[64,1,128]{2,1,0:T(1,128)} %add.3), calls=%async_computation | async-start | bytes 65536 | tf_op jit(solution)/shard_map/all_to_all | solution.py:372
  41.8 16.4 %copy-start.4 = (f32[640]{0:T(1024)S(1)}, f32[640]{0:T(1024)}, u32[]{:S(2)}) copy-start(f32[640]{0:T(1024)} %param.15) | copy-start | bytes 7684
  41.8 16.4 %copy-start.1 = (bf16[640,1920]{1,0:T(8,128)(2,1)S(1)}, bf16[640,1920]{1,0:T(8,128)(2,1)}, u32[]{:S(2)}) copy-start(bf16[640,1920]{1,0:T(8,128)(2,1)} %qkv_ref.4) | copy-start | bytes 7372804
  57.9 2.4 %collective-permute-start.3 = (bf16[512,640]{1,0:T(8,128)(2,1)S(1)}, bf16[512,640]{1,0:T(8,128)(2,1)S(1)}, u32[]{:S(2)}, u32[]{:S(2)}) collective-permute-start(bf16[512,640]{1,0:T(8,128)(2,1)S(1)} %get-tuple-element.12.own_ref), channel_id=1, source_target_pairs={{0,1},{1,0},{2,3},{3,2},{4,5},{5,4},{6,7},{7,6},{8,9},{9,8},{10,11... | collective-permute-start | bytes 1966088 | tf_op jit(solution)/shard_map/ppermute | solution.py:380
  58.2 2.0 %copy-start.3 = (bf16[640,640]{1,0:T(8,128)(2,1)S(1)}, bf16[640,640]{1,0:T(8,128)(2,1)}, u32[]{:S(2)}) copy-start(bf16[640,640]{1,0:T(8,128)(2,1)} %out_ref.1) | copy-start | bytes 2457604
  60.3 53.7 %copy-start.2 = (bf16[640,1920]{1,0:T(8,128)(2,1)S(1)}, bf16[640,1920]{1,0:T(8,128)(2,1)}, u32[]{:S(2)}) copy-start(bf16[640,1920]{1,0:T(8,128)(2,1)} %qkv_ref.5) | copy-start | bytes 7372804
  117.8 43.7 %copy-start = (bf16[640,640]{1,0:T(8,128)(2,1)S(1)}, bf16[640,640]{1,0:T(8,128)(2,1)}, u32[]{:S(2)}) copy-start(bf16[640,640]{1,0:T(8,128)(2,1)} %w_ref.1) | copy-start | bytes 2457604

commit v4 on v3

--- a/solution.py
+++ b/solution.py
@@ -36,13 +36,24 @@
     )
 
 
-def group_slots(channels, offset):
+def group_slots(channels):
     per_group = channels // GROUPS
     slot = lax.broadcasted_iota(jnp.int32, (128, channels), 0)
     chan = lax.broadcasted_iota(jnp.int32, (128, channels), 1)
-    low = (slot - offset) * per_group
-    inside = (chan >= low) & (chan < low + per_group)
-    return jnp.where(inside, 1.0, 0.0).astype(f32)
+    low = (slot % GROUPS) * per_group
+    inside = (chan >= low) & (chan < low + per_group) & (slot < 2 * GROUPS)
+    return jnp.where(inside, 1.0, 0.0).astype(bf16)
+
+
+def pieces(x):
+    high = x.astype(bf16).astype(f32)
+    mid = (x - high).astype(bf16).astype(f32)
+    return [high, mid, x - high - mid]
+
+
+def stacked(first, second):
+    rows = pieces(first) + pieces(second)
+    return jnp.concatenate(rows + [jnp.zeros_like(first)] * 2, axis=0).astype(bf16)
 
 
 def layer_norm(inputs, gain):
@@ -66,15 +77,20 @@
         copy.start()
     first = jnp.zeros((8, channels), f32)
     second = jnp.zeros((8, channels), f32)
-    slots, later = group_slots(channels, 0), group_slots(channels, GROUPS)
+    slots = group_slots(channels)
     for i, copy in enumerate(copies):
         copy.wait()
         x = near[i * tile : i * tile + tile].astype(f32).reshape(tile // 8, 8, channels)
         first += jnp.sum(x, axis=0)
         second += jnp.sum(x * x, axis=0)
-    exact = lax.Precision.HIGHEST
-    total = dot(first, slots, ((1,), (1,)), exact) + dot(second, later, ((1,), (1,)), exact)
-    row = jnp.sum(total, axis=0, keepdims=True)
+    rows = stacked(jnp.sum(first, axis=0, keepdims=True), jnp.sum(second, axis=0, keepdims=True))
+    total = dot(rows, slots, ((1,), (1,)))
+    lane = lax.broadcasted_iota(jnp.int32, (1, 128), 1)
+    row = jnp.where(
+        lane < GROUPS,
+        jnp.sum(total[0:3], axis=0, keepdims=True),
+        jnp.sum(total[3:6], axis=0, keepdims=True),
+    )
     o_ref[...] = jnp.broadcast_to(row[None], o_ref.shape)
 
 
@@ -107,11 +123,18 @@
     @pl.when(first_step)
     def _():
         get_kernel.start()
-        exact = lax.Precision.HIGHEST
-        total = jnp.broadcast_to(jnp.sum(sums_ref[...], axis=0), (8, 128))
-        center = dot(total, group_slots(channels, 0), precision=exact) / number
-        square = dot(total, group_slots(channels, GROUPS), precision=exact) / number
+        total = jnp.sum(sums_ref[...], axis=0)
+        lane = lax.broadcasted_iota(jnp.int32, (1, 128), 1)
+        none = jnp.zeros_like(total)
+        rows = stacked(
+            jnp.where(lane < GROUPS, total, none), jnp.where(lane < GROUPS, none, total)
+        )
+        spread = dot(rows, group_slots(channels))
+        center = jnp.sum(spread[0:3], axis=0, keepdims=True) / number
+        square = jnp.sum(spread[3:6], axis=0, keepdims=True) / number
         scaling = lax.rsqrt(square - center * center + epsilon) * gain_ref[...]
+        scaling = jnp.broadcast_to(scaling, scale.shape[1:])
+        center = jnp.broadcast_to(center, scale.shape[1:])
         scale[0] = scaling
         scale[1] = center
         get_kernel.wait()
@@ -191,7 +214,8 @@
 def project_kernel(own_ref, qkv_ref, queries, keys, values):
     channels = own_ref.shape[1]
     own = own_ref[...]
-    packed = dot(own, qkv_ref[:, :channels]).astype(bf16)
+    factor = 64 ** (-0.5) * LOG2E
+    packed = (dot(own, qkv_ref[:, :channels]) * factor).astype(bf16)
     for j in range(channels // 128):
         queries[j] = packed[:, j * 128 : j * 128 + 128].T
     split_heads(dot(own, qkv_ref[:, channels:]).astype(bf16), keys, values)
@@ -224,14 +248,13 @@
     keys[:, :, :rows] = near_keys[...]
     values[:, :, :rows] = near_values[...]
     split_heads(dot(peer_ref[...], qkv_ref[:, channels:]).astype(bf16), keys, values, rows)
-    factor = 64 ** (-0.5) * LOG2E
     for j in range(pairs):
         q = queries[j]
         parts, weights = [], []
         for part in range(2):
             scores = dot(keys[j, part], q)
             top = jnp.max(scores, axis=0, keepdims=True)
-            weights.append(jnp.exp2((scores - top) * factor).astype(bf16))
+            weights.append(jnp.exp2(scores - top).astype(bf16))
         for part in range(2):
             found = dot(values[j], weights[part])
             parts.append(found[part * 64 : part * 64 + 64] / found[128:129])

time: 164 us -> 162 us (0.988)
  no operation moved by 1% of the time
where the time goes in v4:
time: 162 us
  blocking collectives  88.2 us (54%)
  starting transfers between devices  36.8 us (23%)
  Pallas kernels  23.1 us (14%)
  waiting for transfers between devices  11.7 us (7%)
    all_to_all x1, blocking collectives, body(): lax.all_to_all(normed.reshape(count, pixels // count, channels), FRAME, s...  44.5 us
    all_to_all x1, blocking collectives, body(): lax.all_to_all(result, FRAME, split_axis=0, concat_axis=0, tiled=True)  43.7 us
    ppermute x1, starting transfers between devices, body(): high = lax.ppermute(mine, FRAME, backward)  24.4 us
    all_to_all x1, waiting for transfers between devices, body(): sums = lax.all_to_all(sums, FRAME, split_axis=0, concat_axis=0, tiled=True)  10.4 us
    all_to_all x1, starting transfers between devices, body(): sums = lax.all_to_all(sums, FRAME, split_axis=0, concat_axis=0, tiled=True)  9.99 us
    pallas_call x1, Pallas kernels, space(): pl.pallas_call(space_kernel, out_shape=[jax.ShapeDtypeStruct((rows, chann...  8.62 us
    pallas_call x1, Pallas kernels, front(): pl.pallas_call(functools.partial(front_kernel, number), out_shape=[jax.Sh...  5.64 us
    pallas_call x1, Pallas kernels, time_attend(): pl.pallas_call(time_kernel_body, out_shape=jax.ShapeDtypeStruct(x.shape,...  3.78 us
  transfers between devices with their start and end apart: 5, of which 3 were waited for; matrix products, arithmetic and copies ran while one was open for 1% of the time, Pallas kernels for 2%

profile of v4, /device:TPU:38, one launch (start us, length us, event | category | flops | bytes accessed | tf_op | source)
XLA Modules:
  0.0 162.1 jit_solution(15394261604644838983)
XLA Ops:
  0.0 24.4 %collective-permute-start.2 = (bf16[512,640]{1,0:T(8,128)(2,1)}, bf16[512,640]{1,0:T(8,128)(2,1)S(1)}, u32[]{:S(2)}, u32[]{:S(2)}) collective-permute-start(bf16[512,640]{1,0:T(8,128)(2,1)} %bitcast.8), channel_id=1, source_target_pairs={{2,0},{4,2},{6,4},{8,6},{10,8},{12,10},{14,12},{16,14},{18,16},{20... | collective-permute-start | bytes 1966088 | tf_op jit(solution)/shard_map/ppermute | solution.py:391
  24.4 2.0 %collective-permute-start.1 = (bf16[512,640]{1,0:T(8,128)(2,1)}, bf16[512,640]{1,0:T(8,128)(2,1)}, u32[]{:S(2)}, u32[]{:S(2)}) collective-permute-start(bf16[512,640]{1,0:T(8,128)(2,1)} %bitcast.9), channel_id=1, source_target_pairs={{0,2},{2,4},{4,6},{6,8},{8,10},{10,12},{12,14},{14,16},{16,18},{18... | collective-permute-start | bytes 1966088 | tf_op jit(solution)/shard_map/ppermute | solution.py:390
  26.4 1.4 group_sums.1
  27.8 0.1 collective-permute-start
  28.0 1.2 collective-permute-done
  29.2 0.6 add.3
  29.8 10.0 %all-to-all-start = ((f32[64,1,128]{2,1,0:T(1,128)}), f32[64,1,128]{2,1,0:T(1,128)S(1)}, u32[]{:S(2)}, u32[]{:S(2)}) async-start(f32[64,1,128]{2,1,0:T(1,128)} %add.3), calls=%async_computation | async-start | bytes 65536 | tf_op jit(solution)/shard_map/all_to_all | solution.py:395
  39.8 0.7 reshape.22.gain_ref
  40.5 0.7 reshape.23.norm_ref
  41.2 0.1 add_convert_fusion.edge_ref
  41.3 0.0 copy-start.4
  41.3 0.0 copy-start.1
  41.3 10.4 %all-to-all-done.sums_ref = f32[64,1,128]{2,1,0:T(1,128)S(1)} async-done(((f32[64,1,128]{2,1,0:T(1,128)}), f32[64,1,128]{2,1,0:T(1,128)S(1)}, u32[]{:S(2)}, u32[]{:S(2)}) %all-to-all-start) | async-done | bytes 32800 | tf_op jit(solution)/shard_map/all_to_all | solution.py:395
  51.7 0.0 collective-permute-done.2.high_ref
  51.7 0.0 collective-permute-done.1.low_ref
  51.7 5.6 %front.1 = (f32[512,640]{1,0:T(8,128)S(1)}, bf16[512,640]{1,0:T(8,128)(2,1)S(1)}) custom-call(s32[2]{0:T(128)S(1)} %add_convert_fusion.edge_ref, f32[64,1,128]{2,1,0:T(1,128)S(1)} %all-to-all-done.sums_ref, f32[1,640]{1,0:T(1,128)S(1)} %reshape.22.gain_ref, bf16[512,640]{1,0:T(8,128)(2,1)} %collective-permute-done.1.low_ref, bf16[512,640]{1,0:T(8,128)(2,1)} %bitcast.11, ...), custom_call_target="tpu_custom_call" | custom-call | flops 1258291200 | bytes 4587520 | tf_op jit(solution)/shard_map/front/pallas_call | solution.py:165
  57.3 0.3 collective-permute-start.3
  57.6 0.0 copy-done.4
  57.7 0.0 copy-done.1
  57.7 0.0 copy-start.3
  57.7 1.9 %project.1 = (bf16[5,128,512]{2,1,0:T(8,128)(2,1)S(1)}, bf16[5,2,512,128]{3,2,1,0:T(8,128)(2,1)S(1)}, bf16[5,144,512]{2,1,0:T(8,128)(2,1)S(1)}) custom-call(bf16[512,640]{1,0:T(8,128)(2,1)S(1)} %get-tuple-element.12.own_ref, bf16[640,1920]{1,0:T(8,128)(2,1)S(1)} %copy-done.1), custom_call_target="tpu_custom_call" | custom-call | flops 1258291200 | bytes 2621440 | tf_op jit(solution)/shard_map/project/pallas_call | solution.py:231
  59.6 0.1 collective-permute-done.3.peer_ref
  59.7 0.0 copy-done.3
  59.7 0.0 copy-start.2
  59.7 8.6 %space.1 = (f32[512,640]{1,0:T(8,128)S(1)}, bf16[512,640]{1,0:T(8,128)(2,1)S(1)}) custom-call(bf16[5,128,512]{2,1,0:T(8,128)(2,1)S(1)} %get-tuple-element.13.queries, bf16[5,2,512,128]{3,2,1,0:T(8,128)(2,1)S(1)} %get-tuple-element.14.near_keys, bf16[5,144,512]{2,1,0:T(8,128)(2,1)S(1)} %get-tuple-element.15.near_values, ...), custom_call_target="tpu_custom_call" | custom-call | flops 2600468480 | bytes 4587520 | tf_op jit(solution)/shard_map/space/pallas_call | solution.py:271
  68.3 44.5 %all_to_all.15.x_ref = bf16[64,8,640]{2,1,0:T(8,128)(2,1)S(1)} all-to-all(bf16[64,8,640]{2,1,0:T(8,128)(2,1)S(1)} %bitcast.7), channel_id=1, replica_groups=mesh['groups'=2,'frame'=64,'row'=2] {'frame'}, dimensions={0} | all-to-all | bytes 1310720 | tf_op jit(solution)/shard_map/all_to_all | solution.py:406
  112.9 0.0 copy-done.2
  112.9 3.8 %time_attend.1 = bf16[64,8,640]{2,1,0:T(8,128)(2,1)S(1)} custom-call(bf16[64,8,640]{2,1,0:T(8,128)(2,1)S(1)} %all_to_all.15.x_ref, bf16[640,1920]{1,0:T(8,128)(2,1)S(1)} %copy-done.2), custom_call_target="tpu_custom_call" | custom-call | flops 1929379840 | bytes 1310720 | tf_op jit(solution)/shard_map/time_attend/pallas_call | solution.py:344
  116.6 0.0 copy-start
  116.7 43.7 %all_to_all.16 = bf16[64,8,640]{2,1,0:T(8,128)(2,1)S(1)} all-to-all(bf16[64,8,640]{2,1,0:T(8,128)(2,1)S(1)} %time_attend.1), channel_id=1, replica_groups=mesh['groups'=2,'frame'=64,'row'=2] {'frame'}, dimensions={0} | all-to-all | bytes 1310720 | tf_op jit(solution)/shard_map/all_to_all | solution.py:411
  160.3 0.0 copy-done
  160.3 1.8 %finish.1 = f32[512,640]{1,0:T(8,128)} custom-call(f32[512,640]{1,0:T(8,128)S(1)} %get-tuple-element.17.base_ref, bf16[512,640]{1,0:T(8,128)(2,1)S(1)} %bitcast.6, bf16[640,640]{1,0:T(8,128)(2,1)S(1)} %copy-done), custom_call_target="tpu_custom_call" | custom-call | flops 419430400 | bytes 3276800 | tf_op jit(solution)/shard_map/finish/pallas_call | solution.py:368
  (1 shorter events, 0.0 us)
Async XLA Ops:
  0.0 51.7 %collective-permute-start.2 = (bf16[512,640]{1,0:T(8,128)(2,1)}, bf16[512,640]{1,0:T(8,128)(2,1)S(1)}, u32[]{:S(2)}, u32[]{:S(2)}) collective-permute-start(bf16[512,640]{1,0:T(8,128)(2,1)} %bitcast.8), channel_id=1, source_target_pairs={{2,0},{4,2},{6,4},{8,6},{10,8},{12,10},{14,12},{16,14},{18,16},{20... | collective-permute-start | bytes 1966088 | tf_op jit(solution)/shard_map/ppermute | solution.py:391
  24.4 27.2 %collective-permute-start.1 = (bf16[512,640]{1,0:T(8,128)(2,1)}, bf16[512,640]{1,0:T(8,128)(2,1)}, u32[]{:S(2)}, u32[]{:S(2)}) collective-permute-start(bf16[512,640]{1,0:T(8,128)(2,1)} %bitcast.9), channel_id=1, source_target_pairs={{0,2},{2,4},{4,6},{6,8},{8,10},{10,12},{12,14},{14,16},{16,18},{18... | collective-permute-start | bytes 1966088 | tf_op jit(solution)/shard_map/ppermute | solution.py:390
  27.8 1.3 collective-permute-start
  29.8 21.9 %all-to-all-start = ((f32[64,1,128]{2,1,0:T(1,128)}), f32[64,1,128]{2,1,0:T(1,128)S(1)}, u32[]{:S(2)}, u32[]{:S(2)}) async-start(f32[64,1,128]{2,1,0:T(1,128)} %add.3), calls=%async_computation | async-start | bytes 65536 | tf_op jit(solution)/shard_map/all_to_all | solution.py:395
  41.3 16.4 %copy-start.4 = (f32[640]{0:T(1024)S(1)}, f32[640]{0:T(1024)}, u32[]{:S(2)}) copy-start(f32[640]{0:T(1024)} %param.15) | copy-start | bytes 7684
  41.3 16.4 %copy-start.1 = (bf16[640,1920]{1,0:T(8,128)(2,1)S(1)}, bf16[640,1920]{1,0:T(8,128)(2,1)}, u32[]{:S(2)}) copy-start(bf16[640,1920]{1,0:T(8,128)(2,1)} %qkv_ref.4) | copy-start | bytes 7372804
  57.3 2.4 %collective-permute-start.3 = (bf16[512,640]{1,0:T(8,128)(2,1)S(1)}, bf16[512,640]{1,0:T(8,128)(2,1)S(1)}, u32[]{:S(2)}, u32[]{:S(2)}) collective-permute-start(bf16[512,640]{1,0:T(8,128)(2,1)S(1)} %get-tuple-element.12.own_ref), channel_id=1, source_target_pairs={{0,1},{1,0},{2,3},{3,2},{4,5},{5,4},{6,7},{7,6},{8,9},{9,8},{10,11... | collective-permute-start | bytes 1966088 | tf_op jit(solution)/shard_map/ppermute | solution.py:403
  57.7 2.0 %copy-start.3 = (bf16[640,640]{1,0:T(8,128)(2,1)S(1)}, bf16[640,640]{1,0:T(8,128)(2,1)}, u32[]{:S(2)}) copy-start(bf16[640,640]{1,0:T(8,128)(2,1)} %out_ref.1) | copy-start | bytes 2457604
  59.7 53.1 %copy-start.2 = (bf16[640,1920]{1,0:T(8,128)(2,1)S(1)}, bf16[640,1920]{1,0:T(8,128)(2,1)}, u32[]{:S(2)}) copy-start(bf16[640,1920]{1,0:T(8,128)(2,1)} %qkv_ref.5) | copy-start | bytes 7372804
  116.6 43.7 %copy-start = (bf16[640,640]{1,0:T(8,128)(2,1)S(1)}, bf16[640,640]{1,0:T(8,128)(2,1)}, u32[]{:S(2)}) copy-start(bf16[640,640]{1,0:T(8,128)(2,1)} %w_ref.1) | copy-start | bytes 2457604

commit v5 on v4

--- a/solution.py
+++ b/solution.py
@@ -113,7 +113,7 @@
 
 
 def front_kernel(
-    number, edge_ref, sums_ref, gain_ref, low_ref, mid_ref, high_ref, kernel_far, norm_ref,
+    number, edge_ref, sums_ref, others_ref, gain_ref, low_ref, mid_ref, high_ref, kernel_far, norm_ref,
     stepped_ref, tokens_ref, scale, kernel_ref, sem
 ):
     channels = mid_ref.shape[1]
@@ -123,7 +123,7 @@
     @pl.when(first_step)
     def _():
         get_kernel.start()
-        total = jnp.sum(sums_ref[...], axis=0)
+        total = jnp.sum(sums_ref[...] + others_ref[...], axis=0)
         lane = lax.broadcasted_iota(jnp.int32, (1, 128), 1)
         none = jnp.zeros_like(total)
         rows = stacked(
@@ -157,7 +157,7 @@
     tokens_ref[...] = layer_norm(stepped, norm_ref[...])
 
 
-def front(edge, sums, gain, low, mid, high, time_kernel, norm, number):
+def front(edge, sums, others, gain, low, mid, high, time_kernel, norm, number):
     rows, channels = mid.shape
     tile = rows // 2
     block = pl.BlockSpec((tile, channels), lambda i: (i, 0))
@@ -171,6 +171,7 @@
         grid=(rows // tile,),
         in_specs=[
             pl.BlockSpec(memory_space=pltpu.SMEM),
+            vmem(),
             vmem(),
             one,
             block,
@@ -188,7 +189,7 @@
         compiler_params=params(24),
         cost_estimate=cost(6 * rows * channels * channels, 14 * rows * channels),
         name="front",
-    )(edge, sums, gain, low, pin(mid), high, pin(time_kernel), norm)
+    )(edge, sums, others, gain, low, pin(mid), high, pin(time_kernel), norm)
 
 
 def half_masks(shape):
@@ -391,13 +392,13 @@
     high = lax.ppermute(mine, FRAME, backward)
     members = lax.axis_size(FRAME_ROW)
     sums = group_sums(mine, count)
-    sums += lax.ppermute(sums, "row", [(0, 1), (1, 0)])
     sums = lax.all_to_all(sums, FRAME, split_axis=0, concat_axis=0, tiled=True)
+    others = lax.ppermute(sums, "row", [(0, 1), (1, 0)])
     number = float(members * pixels * (channels // GROUPS))
     here = lax.axis_index(FRAME)
     edge = jnp.stack([here > 0, here < count - 1]).astype(jnp.int32)
     stepped, tokens = front(
-        edge, sums, norm_gain.reshape(1, -1), low, mine, high, time_kernel,
+        edge, sums, others, norm_gain.reshape(1, -1), low, mine, high, time_kernel,
         space_norm.reshape(1, -1), number,
     )
     peer = lax.ppermute(tokens, "row", [(0, 1), (1, 0)])

time: 162 us -> 164 us (1.012)
  transfers between devices with their start and end apart: 5 -> 5, of which waited for: 3 -> 1; matrix products, arithmetic and copies ran while one was open for 1% -> 1% of each run, Pallas kernels for 2% -> 2%
where the time goes in v5:
time: 164 us
  blocking collectives  89.6 us (55%)
  starting transfers between devices  37.2 us (23%)
  Pallas kernels  23.7 us (14%)
  waiting for transfers between devices  11.9 us (7%)
    all_to_all x1, blocking collectives, body(): lax.all_to_all(normed.reshape(count, pixels // count, channels), FRAME, s...  45.9 us
    all_to_all x1, blocking collectives, body(): lax.all_to_all(result, FRAME, split_axis=0, concat_axis=0, tiled=True)  43.7 us
    ppermute x1, starting transfers between devices, body(): high = lax.ppermute(mine, FRAME, backward)  24.4 us
    all_to_all x1, waiting for transfers between devices, body(): sums = lax.all_to_all(sums, FRAME, split_axis=0, concat_axis=0, tiled=True)  11.8 us
    all_to_all x1, starting transfers between devices, body(): sums = lax.all_to_all(sums, FRAME, split_axis=0, concat_axis=0, tiled=True)  10 us
    pallas_call x1, Pallas kernels, space(): pl.pallas_call(space_kernel, out_shape=[jax.ShapeDtypeStruct((rows, chann...  8.61 us
    pallas_call x1, Pallas kernels, front(): pl.pallas_call(functools.partial(front_kernel, number), out_shape=[jax.Sh...  5.65 us
    pallas_call x1, Pallas kernels, time_attend(): pl.pallas_call(time_kernel_body, out_shape=jax.ShapeDtypeStruct(x.shape,...  3.78 us
  transfers between devices with their start and end apart: 5, of which 1 were waited for; matrix products, arithmetic and copies ran while one was open for 1% of the time, Pallas kernels for 2%

profile of v5, /device:TPU:38, one launch (start us, length us, event | category | flops | bytes accessed | tf_op | source)
XLA Modules:
  0.0 164.0 jit_solution(2825689967112556402)
XLA Ops:
  0.0 24.4 %collective-permute-start.2 = (bf16[512,640]{1,0:T(8,128)(2,1)}, bf16[512,640]{1,0:T(8,128)(2,1)S(1)}, u32[]{:S(2)}, u32[]{:S(2)}) collective-permute-start(bf16[512,640]{1,0:T(8,128)(2,1)} %bitcast.8), channel_id=1, source_target_pairs={{2,0},{4,2},{6,4},{8,6},{10,8},{12,10},{14,12},{16,14},{18,16},{20... | collective-permute-start | bytes 1966088 | tf_op jit(solution)/shard_map/ppermute | solution.py:392
  24.4 2.0 %collective-permute-start.1 = (bf16[512,640]{1,0:T(8,128)(2,1)}, bf16[512,640]{1,0:T(8,128)(2,1)S(1)}, u32[]{:S(2)}, u32[]{:S(2)}) collective-permute-start(bf16[512,640]{1,0:T(8,128)(2,1)} %bitcast.9), channel_id=1, source_target_pairs={{0,2},{2,4},{4,6},{6,8},{8,10},{10,12},{12,14},{14,16},{16,18},{18... | collective-permute-start | bytes 1966088 | tf_op jit(solution)/shard_map/ppermute | solution.py:391
  26.4 2.0 %group_sums.1 = f32[64,1,128]{2,1,0:T(1,128)} custom-call(bf16[512,640]{1,0:T(8,128)(2,1)} %bitcast.10), custom_call_target="tpu_custom_call" | custom-call | flops 1310720 | bytes 655360 | tf_op jit(solution)/shard_map/group_sums/pallas_call | solution.py:99
  28.4 10.0 %all-to-all-start = ((f32[64,1,128]{2,1,0:T(1,128)}), f32[64,1,128]{2,1,0:T(1,128)S(1)}, u32[]{:S(2)}, u32[]{:S(2)}) async-start(f32[64,1,128]{2,1,0:T(1,128)} %group_sums.1), calls=%async_computation | async-start | bytes 65536 | tf_op jit(solution)/shard_map/all_to_all | solution.py:395
  38.5 11.8 %all-to-all-done.sums_ref = f32[64,1,128]{2,1,0:T(1,128)S(1)} async-done(((f32[64,1,128]{2,1,0:T(1,128)}), f32[64,1,128]{2,1,0:T(1,128)S(1)}, u32[]{:S(2)}, u32[]{:S(2)}) %all-to-all-start) | async-done | bytes 32800 | tf_op jit(solution)/shard_map/all_to_all | solution.py:395
  50.3 0.0 collective-permute-start
  50.3 0.1 add_convert_fusion.edge_ref
  50.4 0.7 reshape.22.gain_ref
  51.1 0.7 reshape.23.norm_ref
  51.8 0.0 copy-start.4
  51.8 0.0 copy-start.1
  51.8 0.0 collective-permute-done.others_ref
  51.8 0.0 collective-permute-done.2.high_ref
  51.8 0.0 collective-permute-done.1.low_ref
  51.8 5.6 %front.1 = (f32[512,640]{1,0:T(8,128)S(1)}, bf16[512,640]{1,0:T(8,128)(2,1)S(1)}) custom-call(s32[2]{0:T(128)S(1)} %add_convert_fusion.edge_ref, f32[64,1,128]{2,1,0:T(1,128)S(1)} %all-to-all-done.sums_ref, f32[64,1,128]{2,1,0:T(1,128)S(1)} %collective-permute-done.others_ref, f32[1,640]{1,0:T(1,128)S(1)} %reshape.22.gain_ref, ...), custom_call_target="tpu_custom_call" | custom-call | flops 1258291200 | bytes 4587520 | tf_op jit(solution)/shard_map/front/pallas_call | solution.py:165
  57.4 0.8 collective-permute-start.3
  58.3 0.0 copy-done.4
  58.3 0.0 copy-done.1
  58.3 0.0 copy-start.3
  58.3 1.9 %project.1 = (bf16[5,128,512]{2,1,0:T(8,128)(2,1)S(1)}, bf16[5,2,512,128]{3,2,1,0:T(8,128)(2,1)S(1)}, bf16[5,144,512]{2,1,0:T(8,128)(2,1)S(1)}) custom-call(bf16[512,640]{1,0:T(8,128)(2,1)S(1)} %get-tuple-element.12.own_ref, bf16[640,1920]{1,0:T(8,128)(2,1)S(1)} %copy-done.1), custom_call_target="tpu_custom_call" | custom-call | flops 1258291200 | bytes 2621440 | tf_op jit(solution)/shard_map/project/pallas_call | solution.py:232
  60.2 0.0 collective-permute-done.3.peer_ref
  60.2 0.0 copy-done.3
  60.2 0.0 copy-start.2
  60.2 8.6 %space.1 = (f32[512,640]{1,0:T(8,128)S(1)}, bf16[512,640]{1,0:T(8,128)(2,1)S(1)}) custom-call(bf16[5,128,512]{2,1,0:T(8,128)(2,1)S(1)} %get-tuple-element.13.queries, bf16[5,2,512,128]{3,2,1,0:T(8,128)(2,1)S(1)} %get-tuple-element.14.near_keys, bf16[5,144,512]{2,1,0:T(8,128)(2,1)S(1)} %get-tuple-element.15.near_values, ...), custom_call_target="tpu_custom_call" | custom-call | flops 2600468480 | bytes 4587520 | tf_op jit(solution)/shard_map/space/pallas_call | solution.py:272
  68.8 45.9 %all_to_all.15.x_ref = bf16[64,8,640]{2,1,0:T(8,128)(2,1)S(1)} all-to-all(bf16[64,8,640]{2,1,0:T(8,128)(2,1)S(1)} %bitcast.7), channel_id=1, replica_groups=mesh['groups'=2,'frame'=64,'row'=2] {'frame'}, dimensions={0} | all-to-all | bytes 1310720 | tf_op jit(solution)/shard_map/all_to_all | solution.py:407
  114.7 0.0 copy-done.2
  114.7 3.8 %time_attend.1 = bf16[64,8,640]{2,1,0:T(8,128)(2,1)S(1)} custom-call(bf16[64,8,640]{2,1,0:T(8,128)(2,1)S(1)} %all_to_all.15.x_ref, bf16[640,1920]{1,0:T(8,128)(2,1)S(1)} %copy-done.2), custom_call_target="tpu_custom_call" | custom-call | flops 1929379840 | bytes 1310720 | tf_op jit(solution)/shard_map/time_attend/pallas_call | solution.py:345
  118.5 0.0 copy-start
  118.5 43.7 %all_to_all.16 = bf16[64,8,640]{2,1,0:T(8,128)(2,1)S(1)} all-to-all(bf16[64,8,640]{2,1,0:T(8,128)(2,1)S(1)} %time_attend.1), channel_id=1, replica_groups=mesh['groups'=2,'frame'=64,'row'=2] {'frame'}, dimensions={0} | all-to-all | bytes 1310720 | tf_op jit(solution)/shard_map/all_to_all | solution.py:412
  162.2 0.0 copy-done
  162.2 1.8 %finish.1 = f32[512,640]{1,0:T(8,128)} custom-call(f32[512,640]{1,0:T(8,128)S(1)} %get-tuple-element.17.base_ref, bf16[512,640]{1,0:T(8,128)(2,1)S(1)} %bitcast.6, bf16[640,640]{1,0:T(8,128)(2,1)S(1)} %copy-done), custom_call_target="tpu_custom_call" | custom-call | flops 419430400 | bytes 3276800 | tf_op jit(solution)/shard_map/finish/pallas_call | solution.py:369
  (1 shorter events, 0.0 us)
Async XLA Ops:
  0.0 51.8 %collective-permute-start.2 = (bf16[512,640]{1,0:T(8,128)(2,1)}, bf16[512,640]{1,0:T(8,128)(2,1)S(1)}, u32[]{:S(2)}, u32[]{:S(2)}) collective-permute-start(bf16[512,640]{1,0:T(8,128)(2,1)} %bitcast.8), channel_id=1, source_target_pairs={{2,0},{4,2},{6,4},{8,6},{10,8},{12,10},{14,12},{16,14},{18,16},{20... | collective-permute-start | bytes 1966088 | tf_op jit(solution)/shard_map/ppermute | solution.py:392
  24.4 27.3 %collective-permute-start.1 = (bf16[512,640]{1,0:T(8,128)(2,1)}, bf16[512,640]{1,0:T(8,128)(2,1)S(1)}, u32[]{:S(2)}, u32[]{:S(2)}) collective-permute-start(bf16[512,640]{1,0:T(8,128)(2,1)} %bitcast.9), channel_id=1, source_target_pairs={{0,2},{2,4},{4,6},{6,8},{8,10},{10,12},{12,14},{14,16},{16,18},{18... | collective-permute-start | bytes 1966088 | tf_op jit(solution)/shard_map/ppermute | solution.py:391
  28.4 21.9 %all-to-all-start = ((f32[64,1,128]{2,1,0:T(1,128)}), f32[64,1,128]{2,1,0:T(1,128)S(1)}, u32[]{:S(2)}, u32[]{:S(2)}) async-start(f32[64,1,128]{2,1,0:T(1,128)} %group_sums.1), calls=%async_computation | async-start | bytes 65536 | tf_op jit(solution)/shard_map/all_to_all | solution.py:395
  50.3 1.5 collective-permute-start
  51.8 6.5 %copy-start.4 = (f32[640]{0:T(1024)S(1)}, f32[640]{0:T(1024)}, u32[]{:S(2)}) copy-start(f32[640]{0:T(1024)} %param.15) | copy-start | bytes 7684
  51.8 6.5 %copy-start.1 = (bf16[640,1920]{1,0:T(8,128)(2,1)S(1)}, bf16[640,1920]{1,0:T(8,128)(2,1)}, u32[]{:S(2)}) copy-start(bf16[640,1920]{1,0:T(8,128)(2,1)} %qkv_ref.4) | copy-start | bytes 7372804
  57.4 2.7 %collective-permute-start.3 = (bf16[512,640]{1,0:T(8,128)(2,1)S(1)}, bf16[512,640]{1,0:T(8,128)(2,1)S(1)}, u32[]{:S(2)}, u32[]{:S(2)}) collective-permute-start(bf16[512,640]{1,0:T(8,128)(2,1)S(1)} %get-tuple-element.12.own_ref), channel_id=1, source_target_pairs={{0,1},{1,0},{2,3},{3,2},{4,5},{5,4},{6,7},{7,6},{8,9},{9,8},{10,11... | collective-permute-start | bytes 1966088 | tf_op jit(solution)/shard_map/ppermute | solution.py:404
  58.3 1.9 %copy-start.3 = (bf16[640,640]{1,0:T(8,128)(2,1)S(1)}, bf16[640,640]{1,0:T(8,128)(2,1)}, u32[]{:S(2)}) copy-start(bf16[640,640]{1,0:T(8,128)(2,1)} %out_ref.1) | copy-start | bytes 2457604
  60.2 54.5 %copy-start.2 = (bf16[640,1920]{1,0:T(8,128)(2,1)S(1)}, bf16[640,1920]{1,0:T(8,128)(2,1)}, u32[]{:S(2)}) copy-start(bf16[640,1920]{1,0:T(8,128)(2,1)} %qkv_ref.5) | copy-start | bytes 7372804
  118.5 43.7 %copy-start = (bf16[640,640]{1,0:T(8,128)(2,1)S(1)}, bf16[640,640]{1,0:T(8,128)(2,1)}, u32[]{:S(2)}) copy-start(bf16[640,640]{1,0:T(8,128)(2,1)} %w_ref.1) | copy-start | bytes 2457604
